TPU v7x, 32 devices: a 4x4x1 block of a 4x4x8 slice. The times are simulated.
32 devices in a mesh: dp: 1 (over z), sp: 32 (over y, x, core).
Axes of the slice: x: 4, y: 4, z: 1, core: 2. Of those that a mesh axis runs over, the one named last changes fastest.
The devices are a block of a 4x4x8 slice.
Arguments:
- tokens: bfloat16 [64, 5120], P('dp')
- positions: int32 [64], P('dp')
- k_cache: bfloat16 [64, 2048, 8, 128], P('dp', 'sp')
- v_cache: bfloat16 [64, 2048, 8, 128], P('dp', 'sp')
- w_q: bfloat16 [5120, 5120], replicated
- w_k: bfloat16 [5120, 1024], replicated
- w_v: bfloat16 [5120, 1024], replicated
- w_o: bfloat16 [5120, 5120], replicated
- attn_norm: bfloat16 [5120], replicated
- q_norm: bfloat16 [128], replicated
- k_norm: bfloat16 [128], replicated
Outputs:
- output 1: bfloat16 [64, 5120], P('dp')
- output 2: bfloat16 [64, 2048, 8, 128], P('dp', 'sp')
- output 3: bfloat16 [64, 2048, 8, 128], P('dp', 'sp')
- output 4: bfloat16 [64, 2, 8, 128], P('dp')
All inputs are finite; a program needn't handle non-finite values.
Results may differ from a plain program's by a relative error of at most 0.00657234.
Values sent between devices are 32-bit elements.
A program may use at most 768 MiB of HBM per device.

v0:
```python
import jax
import jax.numpy as jnp
from jax import lax
from jax.sharding import PartitionSpec as P

NORM_EPS = 1e-6
ROPE_THETA = 1000000.0
NEG_FILL = -1e30


def rms_scale(values, gain):
    return values * lax.rsqrt(jnp.mean(values * values, axis=-1, keepdims=True) + NORM_EPS) * gain.astype(jnp.float32)


def rope_table(positions, head_dim):
    inv_freq = ROPE_THETA ** (-jnp.arange(head_dim // 2, dtype=jnp.float32) * 2.0 / head_dim)
    angles = positions.astype(jnp.float32)[:, None] * inv_freq[None, :]
    return jnp.cos(angles)[:, None, :], jnp.sin(angles)[:, None, :]


def norm_rope(proj, gain, cos_table, sin_table):
    normed = rms_scale(proj.astype(jnp.float32), gain)
    half_dim = proj.shape[-1] // 2
    first_half = normed[..., :half_dim]
    second_half = normed[..., half_dim:]
    rotated = jnp.concatenate([first_half * cos_table - second_half * sin_table, second_half * cos_table + first_half * sin_table], axis=-1)
    return rotated.astype(jnp.bfloat16)


def project_token(tokens, positions, w_q, w_k, w_v, attn_norm, q_norm, k_norm):
    seq_count = tokens.shape[0]
    head_dim = q_norm.shape[0]
    hidden = rms_scale(tokens.astype(jnp.float32), attn_norm).astype(jnp.bfloat16)
    q_proj = jnp.dot(hidden, w_q, preferred_element_type=jnp.float32).astype(jnp.bfloat16).reshape(seq_count, -1, head_dim)
    k_proj = jnp.dot(hidden, w_k, preferred_element_type=jnp.float32).astype(jnp.bfloat16).reshape(seq_count, -1, head_dim)
    v_new = jnp.dot(hidden, w_v, preferred_element_type=jnp.float32).astype(jnp.bfloat16).reshape(seq_count, -1, head_dim)
    cos_table, sin_table = rope_table(positions, head_dim)
    return norm_rope(q_proj, q_norm, cos_table, sin_table), norm_rope(k_proj, k_norm, cos_table, sin_table), v_new


def local_attention(q_rot, k_rot, v_new, positions, k_loc, v_loc, shard_start):
    seq_count, slot_count, kv_heads, head_dim = k_loc.shape
    q_per_kv = q_rot.shape[1] // kv_heads
    score_scale = head_dim ** -0.5
    slot_ids = shard_start + jnp.arange(slot_count)
    write_mask = (slot_ids[None, :] == positions[:, None])[:, :, None, None]
    k_upd = jnp.where(write_mask, k_rot[:, None], k_loc)
    v_upd = jnp.where(write_mask, v_new[:, None], v_loc)
    q_grp = q_rot.reshape(seq_count, kv_heads, q_per_kv, head_dim)
    scores = jnp.einsum('bkgd,btkd->bkgt', q_grp, k_upd, preferred_element_type=jnp.float32) * score_scale
    live_mask = (slot_ids[None, :] <= positions[:, None])[:, None, None, :]
    local_peak = jnp.max(jnp.where(live_mask, scores, NEG_FILL), axis=-1)
    weights = jnp.where(live_mask, jnp.exp(scores - local_peak[..., None]), 0.0)
    local_sum = jnp.sum(weights, axis=-1)
    local_out = jnp.einsum('bkgt,btkd->bkgd', weights.astype(jnp.bfloat16), v_upd, preferred_element_type=jnp.float32)
    return k_upd, v_upd, local_peak, local_sum, local_out


def solution(mesh):
    cache_spec = P('dp', 'sp', None, None)

    def device_step(tokens, positions, k_cache, v_cache, w_q, w_k, w_v, w_o, attn_norm, q_norm, k_norm):
        q_rot, k_rot, v_new = project_token(tokens, positions, w_q, w_k, w_v, attn_norm, q_norm, k_norm)
        head_dim = q_norm.shape[0]
        shard_start = lax.axis_index('sp') * k_cache.shape[1]
        k_upd, v_upd, local_peak, local_sum, local_out = local_attention(q_rot, k_rot, v_new, positions, k_cache, v_cache, shard_start)
        global_peak = lax.pmax(local_peak, 'sp')
        factor = jnp.exp(local_peak - global_peak)
        packed = jnp.concatenate([local_out * factor[..., None], (local_sum * factor)[..., None]], axis=-1)
        summed = lax.psum(packed, 'sp')
        attn_out = (summed[..., :head_dim] / summed[..., head_dim:]).astype(jnp.bfloat16).reshape(tokens.shape[0], -1)
        block_out = (tokens.astype(jnp.float32) + jnp.dot(attn_out, w_o, preferred_element_type=jnp.float32)).astype(jnp.bfloat16)
        return block_out, k_upd, v_upd, jnp.stack([k_rot, v_new], axis=1)

    return jax.shard_map(device_step, mesh=mesh, in_specs=(P('dp', None), P('dp'), cache_spec, cache_spec, P(), P(), P(), P(), P(), P(), P()), out_specs=(P('dp', None), cache_spec, cache_spec, P('dp', None, None, None)), check_vma=False)
```

profile of v0, /device:TPU:97, one launch (start us, length us, event | category | flops | bytes accessed | tf_op | source)
XLA Modules:
  0.0 262.1 jit_solution(16398704376667802613)
XLA Ops:
  7.2 0.1 all-reduce.2.cloned.1.call-start
  7.3 0.7 convert_element_type.66
  7.9 0.7 convert_element_type.71
  8.6 0.7 convert_element_type.67
  9.3 0.0 slice-start
  9.3 1.5 fusion.12
  10.7 0.7 broadcast_compare_fusion.1
  11.5 0.7 convert_element_type.61
  12.2 0.0 slice-start.1
  12.2 0.0 slice-start.2
  12.2 0.0 copy-start.1
  12.2 6.3 %fusion.18 = bf16[8,8,8,128]{3,1,2,0:T(8,128)(2,1)S(1)} fusion(bf16[5120,1024]{1,0:T(8,128)(2,1)} %param.17, bf16[64,5120]{1,0:T(8,128)(2,1)} %param.11, f32[5120]{0:T(1024)S(1)} %convert_element_type.61, f32[64]{0:T(128)S(1)} %add_rsqrt_fusion.2), kind=kOutput, calls=%fused_computation.32 | convolution fusion | flops 672464896 | bytes 11292928 | tf_op jit(solution)/shard_map/dot_general | solution.py:36
  18.6 0.0 slice-done
  18.6 0.0 slice-done.1
  18.6 0.0 slice-done.2
  18.6 0.0 copy-done.1
  18.6 2.0 fusion.17
  20.7 0.1 multiply_reduce_fusion.1
  20.8 0.1 copy.60
  20.9 0.1 copy.61
  21.0 20.9 %fusion.5 = f32[64,5120]{1,0:T(8,128)S(1)} fusion(bf16[5120,5120]{1,0:T(8,128)(2,1)} %param.15, bf16[64,5120]{1,0:T(8,128)(2,1)S(1)} %copy-done.1, f32[5120]{0:T(1024)S(1)} %convert_element_type.61, f32[64]{0:T(128)S(1)} %add_rsqrt_fusion.2), kind=kOutput, calls=%fused_computation.9 | convolution fusion | flops 3357409280 | bytes 54415616 | tf_op jit(solution)/shard_map/dot_general | solution.py:34
  41.9 0.2 copy.74
  42.1 0.4 multiply_reduce_fusion
  42.5 0.1 copy.56
  42.6 0.2 multiply_cosine_fusion
  42.8 0.1 multiply_multiply_fusion
  43.0 0.4 fusion.15
  43.4 0.2 subtract_convert_fusion.1
  43.5 0.6 subtract_convert_fusion
  44.1 0.5 copy.59
  44.6 0.5 copy.58
  45.1 0.1 pad_maximum_fusion.2
  45.2 9.5 %broadcast_select_fusion = (bf16[64,64,8,128]{3,2,1,0:T(8,128)(2,1)}, bf16[64,64,8,128]{3,2,1,0:T(8,128)(2,1)S(1)}) fusion(bf16[64,64,8,128]{3,2,1,0:T(8,128)(2,1)} %param.14, pred[64,64]{1,0:T(8,128)(4,1)S(1)} %get-tuple-element.13, bf16[64,8,128]{2,1,0:T(8,128)(2,1)S(1)} %bitcast.44, bf16[64,64,8,128]{3,2,1,0:T(8,128)(2,1)} %param.13, ...), kind=kLoop, calls=%fused_computation.4 | loop fusion | flops 8388608 | bytes 33820672 | tf_op jit(solution)/shard_map/jit(_where)/select_n | solution.py:48
  54.6 0.0 copy-start
  54.7 4.7 %select_reduce_fusion = (f32[64,8,5]{2,1,0:T(8,128)S(1)}, f32[64,8,5,64]{3,2,1,0:T(8,128)S(1)}) fusion(pred[64,64]{1,0:T(8,128)(4,1)S(1)} %get-tuple-element.12, bf16[64,64,8,128]{3,2,1,0:T(8,128)(2,1)S(1)} %get-tuple-element.11, bf16[64,8,5,64]{3,2,1,0:T(8,128)(2,1)S(1)} %copy.59, bf16[64,8,5,64]{3,2,1,0:T(8,128)(2,1)S(1)} %copy.58), kind=kOutput, calls=%fused_computation.14 | convolution fusion | flops 43742720 | bytes 9713664 | tf_op jit(solution)/shard_map/bkgd,btkd->bkgt/dot_general | solution.py:50
  59.4 0.0 copy-done
  59.4 51.5 %pmax.7 = f32[64,8,5]{2,1,0:T(8,128)} all-reduce(f32[64,8,5]{2,1,0:T(8,128)S(1)} %get-tuple-element.16), channel_id=1, replica_groups=mesh['dp'=1,'sp'=32] {'sp'}, use_global_device_ids=true, to_apply=%region_4.5 | all-reduce | flops 2560 | bytes 20480 | tf_op jit(solution)/shard_map/pmax | solution.py:67
  110.9 0.0 copy-start.3
  110.9 1.3 fusion.7
  112.3 0.0 copy-done.3
  112.3 0.8 multiply_bitcast_fusion
  113.1 5.4 %copy.65 = f32[64,8,5,1]{3,2,1,0:T(8,128)} copy(f32[64,8,5,1]{2,1,0,3:T(8,128)} %get-tuple-element.4) | data formatting | bytes 20480 | tf_op jit(solution)/shard_map/broadcast_in_dim | solution.py:69
  118.5 0.0 copy-start.2
  118.5 5.7 %fusion.9 = f32[64,8,5,128]{3,2,1,0:T(8,128)S(1)} fusion(bf16[64,64,8,128]{3,2,1,0:T(8,128)(2,1)} %get-tuple-element.10, f32[64,8,5,64]{3,2,1,0:T(8,128)S(1)} %get-tuple-element.17, f32[64,8,5]{2,1,0:T(8,128)} %get-tuple-element.5, f32[64,8,5]{2,1,0:T(8,128)S(1)} %get-tuple-element.16, pred[64,64]{1,0:T(8,128)(4,1)S(1)} %get-tuple-element.12), kind=kOutput, calls=%fused_computation.19 | convolution fusion | flops 42926080 | bytes 10379264 | tf_op jit(solution)/shard_map/bkgt,btkd->bkgd/dot_general | solution.py:55
  124.2 0.0 copy-done.2
  124.2 2.5 pad_maximum_fusion
  126.8 0.1 all-reduce.2.cloned.1.call-update
  126.8 0.8 pad_maximum_fusion.1
  127.6 98.7 %all-reduce.2.cloned.1.call-done = f32[64,8,5,129]{3,2,1,0:T(8,128)} async-done(((f32[64,8,5,129]{3,2,1,0:T(8,128)}), f32[64,8,5,129]{3,2,1,0:T(8,128)}) %all-reduce.2.cloned.1.call-update) | async-done | bytes 1320976 | tf_op jit(solution)/shard_map/psum | solution.py:70
  226.3 0.0 slice-start.3
  226.3 1.6 slice-done.3
  227.9 3.1 %copy.72 = f32[64,8,5,1]{2,1,0,3:T(8,128)S(1)} copy(f32[64,8,5,1]{3,2,1,0:T(8,128)S(1)} %slice-done.3) | data formatting | bytes 20480 | tf_op jit(solution)/shard_map/div | solution.py:71
  231.0 2.0 fusion.6
  233.0 0.7 reshape.191
  233.7 21.5 %fusion.4 = bf16[64,5120]{1,0:T(8,128)(2,1)} fusion(bf16[64,5120]{1,0:T(8,128)(2,1)S(1)} %reshape.191, bf16[5120,5120]{1,0:T(8,128)(2,1)} %param.18, bf16[64,5120]{1,0:T(8,128)(2,1)S(1)} %copy-done.1), kind=kOutput, calls=%fused_computation.7 | convolution fusion | flops 3356426240 | bytes 54394880 | tf_op jit(solution)/shard_map/dot_general | solution.py:72
  (8 shorter events, 0.1 us)
Async XLA Ops:
  7.2 219.1 %all-reduce.2.cloned.1.call-start = ((), (), s32[]{:S(2)}) async-start(), calls=%async_computation | async-start | bytes 8388608 | tf_op jit(solution)/shard_map/psum | solution.py:70
  9.3 9.3 %slice-start = ((s8[10485760]{0:T(1024)(128)(4,1)}), s8[4194304]{0:T(1024)(128)(4,1)S(1)}, s32[]{:S(2)}) async-start(s8[10485760]{0:T(1024)(128)(4,1)} %bitcast.37), calls=%async_computation.1 | async-start | bytes 8388608
  12.2 6.4 %slice-start.1 = ((s8[10485760]{0:T(1024)(128)(4,1)}), s8[4194304]{0:T(1024)(128)(4,1)S(1)}, s32[]{:S(2)}) async-start(s8[10485760]{0:T(1024)(128)(4,1)} %bitcast.37), calls=%async_computation.2 | async-start | bytes 8388608
  12.2 6.4 %slice-start.2 = ((s8[10485760]{0:T(1024)(128)(4,1)}), s8[2097152]{0:T(1024)(128)(4,1)S(1)}, s32[]{:S(2)}) async-start(s8[10485760]{0:T(1024)(128)(4,1)} %bitcast.37), calls=%async_computation.3 | async-start | bytes 4194304
  12.2 6.4 %copy-start.1 = (bf16[64,5120]{1,0:T(8,128)(2,1)S(1)}, bf16[64,5120]{1,0:T(8,128)(2,1)}, u32[]{:S(2)}) copy-start(bf16[64,5120]{1,0:T(8,128)(2,1)} %param.11) | copy-start | bytes 1966084
  54.6 4.7 %copy-start = (bf16[64,64,8,128]{3,2,1,0:T(8,128)(2,1)}, bf16[64,64,8,128]{3,2,1,0:T(8,128)(2,1)S(1)}, u32[]{:S(2)}) copy-start(bf16[64,64,8,128]{3,2,1,0:T(8,128)(2,1)S(1)} %get-tuple-element.11) | copy-start | bytes 25165828
  110.9 1.4 copy-start.3
  118.5 5.7 %copy-start.2 = (f32[64,8,5,1]{3,2,1,0:T(8,128)S(1)}, f32[64,8,5,1]{3,2,1,0:T(8,128)}, u32[]{:S(2)}) copy-start(f32[64,8,5,1]{3,2,1,0:T(8,128)} %copy.65) | copy-start | bytes 30724
  226.3 1.6 slice-start.3
Sparse Core Ops, SparseCore 0:
  126.9 99.3 all-reduce.1
where the time goes:
time: 262 us
  waiting for transfers between devices  98.7 us (38%)
  matrix products  61.1 us (23%)
  blocking collectives  51.5 us (20%)
  other arithmetic  24 us (9%)
  between operations  14.3 us (5%)
  local copies, waits for them, and re-layouts  12.4 us (5%)
    psum x1, waiting for transfers between devices, device_step(): summed = lax.psum(packed, 'sp')  98.7 us
    pmax x1, blocking collectives, device_step(): global_peak = lax.pmax(local_peak, 'sp')  51.5 us
    dot_general x1, matrix products, device_step(): jnp.dot(attn_out, w_o, preferred_element_type=jnp.float32)  21.5 us
    dot_general x1, matrix products, project_token(): jnp.dot(hidden, w_q, preferred_element_type=jnp.float32)  20.9 us
    select_n x1, other arithmetic, local_attention(): v_upd = jnp.where(write_mask, v_new[:, None], v_loc)  9.47 us
    dot_general x1, matrix products, project_token(): jnp.dot(hidden, w_v, preferred_element_type=jnp.float32)  6.32 us
    dot_general x1, matrix products, local_attention(): jnp.einsum('bkgt,btkd->bkgd', weights.astype(jnp.bfloat16), v_upd, prefer...  5.68 us
    broadcast_in_dim x1, local copies, waits for them, and re-layouts, device_step(): (local_sum * factor)[..., None]  5.42 us
  transfers between devices with their start and end apart: 1, of which 1 were waited for; matrix products, arithmetic and copies ran while one was open for 0% of the time, Pallas kernels for 0%

commit v1 on v0

v1 whole, which is shorter than its diff:
```python
import functools

import jax
import jax.numpy as jnp
from jax import lax
from jax.experimental import pallas as pl
from jax.experimental.pallas import tpu as pltpu
from jax.sharding import PartitionSpec as P

NORM_EPS = 1e-6
ROPE_THETA = 1000000.0
NEG_FILL = -1e30
MESH = pl.DeviceIdType.MESH
F32 = jnp.float32
BF16 = jnp.bfloat16


def rms_scale(values, gain):
    return values * lax.rsqrt(jnp.mean(values * values, axis=-1, keepdims=True) + NORM_EPS) * gain.astype(F32)


def rope_table(positions, head_dim):
    inv_freq = ROPE_THETA ** (-jnp.arange(head_dim // 2, dtype=F32) * 2.0 / head_dim)
    angles = positions.astype(F32)[:, None] * inv_freq[None, :]
    return jnp.cos(angles)[:, None, :], jnp.sin(angles)[:, None, :]


def norm_rope(proj, gain, cos_table, sin_table):
    normed = rms_scale(proj.astype(F32), gain)
    half_dim = proj.shape[-1] // 2
    first_half = normed[..., :half_dim]
    second_half = normed[..., half_dim:]
    rotated = jnp.concatenate([first_half * cos_table - second_half * sin_table, second_half * cos_table + first_half * sin_table], axis=-1)
    return rotated.astype(BF16)


def project_token(tokens, positions, w_q, w_k, w_v, attn_norm, q_norm, k_norm):
    seq_count = tokens.shape[0]
    head_dim = q_norm.shape[0]
    hidden = rms_scale(tokens.astype(F32), attn_norm).astype(BF16)
    q_proj = jnp.dot(hidden, w_q, preferred_element_type=F32).astype(BF16).reshape(seq_count, -1, head_dim)
    k_proj = jnp.dot(hidden, w_k, preferred_element_type=F32).astype(BF16).reshape(seq_count, -1, head_dim)
    v_new = jnp.dot(hidden, w_v, preferred_element_type=F32).astype(BF16).reshape(seq_count, -1, head_dim)
    cos_table, sin_table = rope_table(positions, head_dim)
    return norm_rope(q_proj, q_norm, cos_table, sin_table), norm_rope(k_proj, k_norm, cos_table, sin_table), v_new


def attn_body(seqs, slots, kv_heads, q_heads, pos_ref, start_ref, q_ref, kv_ref, k_ref, v_ref, ko_ref, vo_ref, o_ref, ml_ref):
    head_dim = q_ref.shape[-1]
    step = pl.program_id(0)
    scale = head_dim ** -0.5
    cols = slots * kv_heads
    group = q_heads // kv_heads
    row_id = lax.broadcasted_iota(jnp.int32, (q_heads, cols), 0)
    col_id = lax.broadcasted_iota(jnp.int32, (q_heads, cols), 1)
    own_head = jnp.zeros((q_heads, cols), jnp.int32)
    for h in range(1, kv_heads):
        own_head += (row_id >= h * group).astype(jnp.int32)
    slot_of = jnp.where(lax.rem(col_id, kv_heads) == own_head, lax.div(col_id, kv_heads), 1 << 20)
    upper = lax.broadcasted_iota(jnp.int32, (2 * kv_heads, head_dim), 0) >= kv_heads
    diag_r = lax.broadcasted_iota(jnp.int32, (q_heads, head_dim), 0)
    diag_c = lax.broadcasted_iota(jnp.int32, (q_heads, head_dim), 1)
    diag = diag_r == diag_c
    for b in range(seqs):
        rel = pos_ref[step * seqs + b] - start_ref[0]
        ko_ref[b] = k_ref[b]
        vo_ref[b] = v_ref[b]

        @pl.when((rel >= 0) & (rel < slots))
        def _():
            tile = lax.div(rel, 2)
            hit = upper == (lax.rem(rel, 2) == 1)
            k_new = kv_ref[pl.ds(b * 2 * kv_heads, kv_heads), :]
            v_new = kv_ref[pl.ds(b * 2 * kv_heads + kv_heads, kv_heads), :]
            k_two = jnp.concatenate([k_new, k_new], axis=0)
            v_two = jnp.concatenate([v_new, v_new], axis=0)
            ko_ref[b, tile] = jnp.where(hit, k_two, ko_ref[b, tile].astype(F32)).astype(BF16)
            vo_ref[b, tile] = jnp.where(hit, v_two, vo_ref[b, tile].astype(F32)).astype(BF16)

    for b in range(seqs):
        rel = pos_ref[step * seqs + b] - start_ref[0]
        keys = ko_ref[b].reshape(cols, head_dim)
        vals = vo_ref[b].reshape(cols, head_dim)
        query = q_ref[pl.ds(b * q_heads, q_heads), :].astype(BF16)
        scores = lax.dot_general(query, keys, (((1,), (1,)), ((), ())), preferred_element_type=F32) * scale
        live = slot_of <= rel
        scores = jnp.where(live, scores, NEG_FILL)
        peak = jnp.max(scores, axis=1, keepdims=True)
        weights = jnp.where(live, jnp.exp(scores - peak), 0.0)
        total = jnp.sum(weights, axis=1, keepdims=True)
        o_ref[pl.ds(b * q_heads, q_heads), :] = jnp.dot(weights.astype(BF16), vals, preferred_element_type=F32)
        ml_ref[0, 0, pl.ds(b, 1), :] = jnp.sum(jnp.where(diag, peak, 0.0), axis=0, keepdims=True)
        ml_ref[0, 1, pl.ds(b, 1), :] = jnp.sum(jnp.where(diag, total, 0.0), axis=0, keepdims=True)


def attention(q_rows, kv_rows, positions, shard_start, k_cache, v_cache):
    seq_count, slots, kv_heads, head_dim = k_cache.shape
    q_heads = q_rows.shape[0] // seq_count
    seqs = 8
    steps = seq_count // seqs
    pairs = slots // 2
    k4 = k_cache.reshape(seq_count, pairs, 2 * kv_heads, head_dim)
    v4 = v_cache.reshape(seq_count, pairs, 2 * kv_heads, head_dim)
    cache_block = pl.BlockSpec((seqs, pairs, 2 * kv_heads, head_dim), lambda i, *_: (i, 0, 0, 0))
    grid_spec = pltpu.PrefetchScalarGridSpec(
        num_scalar_prefetch=2,
        grid=(steps,),
        in_specs=[
            pl.BlockSpec((seqs * q_heads, head_dim), lambda i, *_: (i, 0)),
            pl.BlockSpec((seqs * 2 * kv_heads, head_dim), lambda i, *_: (i, 0)),
            cache_block,
            cache_block,
        ],
        out_specs=[
            cache_block,
            cache_block,
            pl.BlockSpec((seqs * q_heads, head_dim), lambda i, *_: (i, 0)),
            pl.BlockSpec((1, 2, seqs, head_dim), lambda i, *_: (i, 0, 0, 0)),
        ],
    )
    k_out, v_out, part, ml = pl.pallas_call(
        functools.partial(attn_body, seqs, slots, kv_heads, q_heads),
        grid_spec=grid_spec,
        out_shape=[
            jax.ShapeDtypeStruct(k4.shape, BF16),
            jax.ShapeDtypeStruct(v4.shape, BF16),
            jax.ShapeDtypeStruct((seq_count * q_heads, head_dim), F32),
            jax.ShapeDtypeStruct((steps, 2, seqs, head_dim), F32),
        ],
        compiler_params=pltpu.CompilerParams(dimension_semantics=("arbitrary",)),
        name="attend",
    )(positions, shard_start, q_rows, kv_rows, k4, v4)
    return k_out.reshape(k_cache.shape), v_out.reshape(v_cache.shape), part, ml


def blend(parts, stats, seqs, q_heads, row0=0):
    peak = stats[0][0]
    for m, _ in stats[1:]:
        peak = jnp.maximum(peak, m)
    factors = [jnp.exp(m - peak) for m, _ in stats]
    total = factors[0] * stats[0][1]
    for f, (_, l) in zip(factors[1:], stats[1:]):
        total += f * l
    return peak, total, factors


def columns_of(tile):
    return jnp.transpose(tile)


def combine_body(side, q_heads, o_ref, ml_ref, tok_ref, wo_ref, out_ref,
                 r1, rm1, s1, sm1, r2, rm2, s2, sm2, r3, rm3, obuf, lhs, wbuf, gbuf, acc,
                 w_sem, a_s, a_r, b_s, b_r, c_s, c_r, d_s, d_r, e_s, e_r, f_s, f_r, h_s, h_r):
    me = lax.axis_index("sp")
    core = lax.rem(me, 2)
    chip = lax.div(me, 2)
    x = lax.rem(chip, side)
    y = lax.div(chip, side)
    first = x * (1 - core) + y * core
    second = y * (1 - core) + x * core
    stride1 = 2 * (1 - core) + 2 * side * core
    stride2 = 2 * side * (1 - core) + 2 * core
    partner = me + 1 - 2 * core
    head_dim = o_ref.shape[-1]
    width = wbuf.shape[1]
    depth = wbuf.shape[0]
    w_parts = w_sem.shape[0]
    w_rows = depth // w_parts
    order = [side // 2] + [d for d in range(1, side) if d != side // 2]

    def peer1(d):
        return me + (lax.rem(first + d, side) - first) * stride1

    def peer2(d):
        return me + (lax.rem(second + d, side) - second) * stride2

    def send(src, dst, ssem, rsem, to):
        copy = pltpu.make_async_remote_copy(src_ref=src, dst_ref=dst, send_sem=ssem, recv_sem=rsem, device_id={"sp": to}, device_id_type=MESH)
        copy.start()
        return copy

    w_copies = []
    for i in range(w_parts):
        copy = pltpu.make_async_copy(
            wo_ref.at[pl.ds(i * w_rows, w_rows), pl.ds(pl.multiple_of(core * width, 128), width)],
            wbuf.at[pl.ds(i * w_rows, w_rows), :], w_sem.at[i])
        copy.start()
        w_copies.append(copy)

    barrier = pltpu.get_barrier_semaphore()
    neighbours = [partner] + [peer1(d) for d in range(1, side)] + [peer2(d) for d in range(1, side)]
    for n in neighbours:
        pl.semaphore_signal(barrier, inc=1, device_id={"sp": n}, device_id_type=MESH)
    pl.semaphore_wait(barrier, len(neighbours))

    started = []
    in1 = {}
    for d in order + [0]:
        piece = lax.rem(second + d, side)
        in1[d] = (send(o_ref.at[1 - core, piece], r1.at[d], a_s.at[d, 0], a_r.at[d, 0], partner),
                  send(ml_ref.at[1 - core, piece], rm1.at[d], a_s.at[d, 1], a_r.at[d, 1], partner))
    in2 = {}
    for d in order + [0]:
        in1[d][0].wait_recv()
        in1[d][1].wait_recv()
        piece = lax.rem(first + d, side)
        own_m, own_l = ml_ref[core, piece, 0], ml_ref[core, piece, 1]
        peak, total, fac = blend(None, [(own_m, own_l), (rm1[d, 0], rm1[d, 1])], None, None)
        sm1[d, 0] = peak
        sm1[d, 1] = total
        cols = [columns_of(f) for f in fac]
        for k in range(side):
            for i in range(2):
                seq = 2 * k + i
                rows = pl.ds(i * q_heads, q_heads)
                s1[d, k, rows, :] = (o_ref[core, piece, k, rows, :] * cols[0][:q_heads, seq:seq + 1]
                                     + r1[d, k, rows, :] * cols[1][:q_heads, seq:seq + 1])
        if d:
            in2[d] = (send(s1.at[d], r2.at[d], b_s.at[d, 0], b_r.at[d, 0], peer1(d)),
                      send(sm1.at[d], rm2.at[d], b_s.at[d, 1], b_r.at[d, 1], peer1(d)))
    for d in order:
        in2[d][0].wait_recv()
        in2[d][1].wait_recv()
    stats = [(sm1[0, 0], sm1[0, 1])] + [(rm2[d, 0], rm2[d, 1]) for d in range(1, side)]
    peak, total, fac = blend(None, stats, None, None)
    sm2[0] = peak
    sm2[1] = total
    cols = [columns_of(f) for f in fac]
    for k in range(side):
        for i in range(2):
            seq = 2 * k + i
            rows = pl.ds(i * q_heads, q_heads)
            value = s1[0, k, rows, :] * cols[0][:q_heads, seq:seq + 1]
            for d in range(1, side):
                value += r2[d, k, rows, :] * cols[d][:q_heads, seq:seq + 1]
            s2[k, rows, :] = value
    in3 = {}
    for d in order:
        in3[d] = (send(s2.at[lax.rem(second + d, side)], r3.at[d], c_s.at[d, 0], c_r.at[d, 0], peer2(d)),
                  send(sm2, rm3.at[d], c_s.at[d, 1], c_r.at[d, 1], peer2(d)))
    for d in order:
        in3[d][0].wait_recv()
        in3[d][1].wait_recv()
    stats = [(sm2[0], sm2[1])] + [(rm3[d, 0], rm3[d, 1]) for d in range(1, side)]
    peak, total, fac = blend(None, stats, None, None)
    rm3[0, 0] = total
    for d in range(side):
        rm3[d, 1] = fac[d]
    mine = pl.ds(2 * second, 2)
    cols = []
    for d in range(side):
        cols.append(columns_of(jnp.concatenate([rm3[d, 1, mine, :]] * 4, axis=0)))
    l_cols = columns_of(jnp.concatenate([rm3[0, 0, mine, :]] * 4, axis=0))
    for i in range(2):
        rows = pl.ds(i * q_heads, q_heads)
        value = s2[second, rows, :] * cols[0][:q_heads, i:i + 1]
        for d in range(1, side):
            value += r3[d, rows, :] * cols[d][:q_heads, i:i + 1]
        value = value / l_cols[:q_heads, i:i + 1]
        obuf[core, rows, :] = value.astype(BF16).astype(F32)
    swap = send(obuf.at[core], obuf.at[core], d_s, d_r, partner)
    swap.wait_recv()

    for i in range(2):
        for h in range(q_heads):
            lhs[i:i + 1, h * head_dim:(h + 1) * head_dim] = obuf[0, i * q_heads + h:i * q_heads + h + 1, :]
            lhs[2 + i:3 + i, h * head_dim:(h + 1) * head_dim] = obuf[1, i * q_heads + h:i * q_heads + h + 1, :]
    for copy in w_copies:
        copy.wait()
    left = lhs[...].astype(BF16)

    def pair_a(f, s):
        return (f * side + s) * (1 - core) + (s * side + f) * core

    def pair_b(f, s):
        return side * side + (s * side + f) * (1 - core) + (f * side + s) * core

    pa, pb = pair_a(first, second), pair_b(first, second)
    n_step = 512
    for n in range(0, width, n_step):
        prod = jnp.dot(left, wbuf[:, n:n + n_step], preferred_element_type=F32)
        gbuf[core, pa, :, n:n + n_step] = prod[0:2]
        gbuf[core, pb, :, n:n + n_step] = prod[2:4]

    g1, g2, g3 = {}, {}, {}
    for d in order:
        for ab, p in enumerate((pa, pb)):
            g1[d, ab] = send(gbuf.at[core, p], gbuf.at[core, p], e_s.at[d, ab], e_r.at[d, ab], peer1(d))
    for ab, p in enumerate((pa, pb)):
        for e in order:
            g2[e, 0, ab] = send(gbuf.at[core, p], gbuf.at[core, p], f_s.at[e, 0, ab], f_r.at[e, 0, ab], peer2(e))
        g3[0, 0, ab] = send(gbuf.at[core, p], gbuf.at[core, p], h_s.at[0, 0, ab], h_r.at[0, 0, ab], partner)
    for d in order:
        f_from = lax.rem(first - d + side, side)
        for ab, p in enumerate((pair_a(f_from, second), pair_b(f_from, second))):
            g1[d, ab].wait_recv()
            for e in order:
                g2[e, d, ab] = send(gbuf.at[core, p], gbuf.at[core, p], f_s.at[e, d, ab], f_r.at[e, d, ab], peer2(e))
            g3[0, d, ab] = send(gbuf.at[core, p], gbuf.at[core, p], h_s.at[0, d, ab], h_r.at[0, d, ab], partner)
    for d in [0] + order:
        f_from = lax.rem(first - d + side, side)
        for e in order:
            s_from = lax.rem(second - e + side, side)
            for ab, p in enumerate((pair_a(f_from, s_from), pair_b(f_from, s_from))):
                g2[e, d, ab].wait_recv()
                g3[e, d, ab] = send(gbuf.at[core, p], gbuf.at[core, p], h_s.at[e, d, ab], h_r.at[e, d, ab], partner)
    for key in g3:
        g3[key].wait_recv()
    for half in range(2):
        for p in range(2 * side * side):
            acc[2 * p:2 * p + 2, half * width:(half + 1) * width] = gbuf[half, p]
    out_ref[...] = (tok_ref[...].astype(F32) + acc[...]).astype(BF16)

    for group in (in1, in2, in3):
        for pair in group.values():
            pair[0].wait_send()
            pair[1].wait_send()
    swap.wait_send()
    for group in (g1, g2, g3):
        for copy in group.values():
            copy.wait_send()


def combine(part, ml, tokens, w_o, side):
    seq_count, dim = tokens.shape
    head_dim = part.shape[-1]
    q_heads = part.shape[0] // seq_count
    rows = 2 * q_heads
    o5 = part.reshape(2, side, side, rows, head_dim)
    m5 = ml.reshape(2, side, 2, ml.shape[2], head_dim)
    width = dim // 2
    depth = w_o.shape[0]
    dma = pltpu.SemaphoreType.DMA
    vmem = pl.BlockSpec(memory_space=pltpu.VMEM)
    piece = (side, side, rows, head_dim)
    stat = (side, 2, ml.shape[2], head_dim)
    return pl.pallas_call(
        functools.partial(combine_body, side, q_heads),
        out_shape=jax.ShapeDtypeStruct(tokens.shape, BF16),
        in_specs=[vmem, vmem, vmem, pl.BlockSpec(memory_space=pl.ANY)],
        out_specs=vmem,
        scratch_shapes=[
            pltpu.VMEM(piece, F32), pltpu.VMEM(stat, F32),
            pltpu.VMEM(piece, F32), pltpu.VMEM(stat, F32),
            pltpu.VMEM(piece, F32), pltpu.VMEM(stat, F32),
            pltpu.VMEM(piece[1:], F32), pltpu.VMEM(stat[1:], F32),
            pltpu.VMEM(piece[1:], F32), pltpu.VMEM(stat, F32),
            pltpu.VMEM((2, rows, head_dim), F32),
            pltpu.VMEM((8, depth), F32),
            pltpu.VMEM((depth, width), BF16),
            pltpu.VMEM((2, 2 * side * side, 2, width), F32),
            pltpu.VMEM(tokens.shape, F32),
            dma((4,)),
            dma((side, 2)), dma((side, 2)),
            dma((side, 2)), dma((side, 2)),
            dma((side, 2)), dma((side, 2)),
            dma, dma,
            dma((side, 2)), dma((side, 2)),
            dma((side, side, 2)), dma((side, side, 2)),
            dma((side, side, 2)), dma((side, side, 2)),
        ],
        compiler_params=pltpu.CompilerParams(collective_id=1, has_side_effects=True, vmem_limit_bytes=60 * 1024 * 1024),
        name="combine",
    )(o5, m5, tokens, w_o)


def solution(mesh):
    cache_spec = P('dp', 'sp', None, None)
    side = int(round((mesh.shape['sp'] // 2) ** 0.5))

    def device_step(tokens, positions, k_cache, v_cache, w_q, w_k, w_v, w_o, attn_norm, q_norm, k_norm):
        q_rot, k_rot, v_new = project_token(tokens, positions, w_q, w_k, w_v, attn_norm, q_norm, k_norm)
        head_dim = q_norm.shape[0]
        new_kv = jnp.stack([k_rot, v_new], axis=1)
        shard_start = (lax.axis_index('sp') * k_cache.shape[1]).astype(jnp.int32).reshape(1)
        q_rows = q_rot.astype(F32).reshape(-1, head_dim)
        kv_rows = new_kv.astype(F32).reshape(-1, head_dim)
        k_upd, v_upd, part, ml = attention(q_rows, kv_rows, positions, shard_start, k_cache, v_cache)
        block_out = combine(part, ml, tokens, w_o, side)
        return block_out, k_upd, v_upd, new_kv

    return jax.shard_map(device_step, mesh=mesh, in_specs=(P('dp', None), P('dp'), cache_spec, cache_spec, P(), P(), P(), P(), P(), P(), P()), out_specs=(P('dp', None), cache_spec, cache_spec, P('dp', None, None, None)), check_vma=False)
```

time: 262 us -> 101 us (0.39)
  waiting for transfers between devices: 98.7 us -> 0 us
  Pallas kernels: 0 us -> 60 us
  blocking collectives: 51.5 us -> 0 us
  matrix products: 61.1 us -> 28.8 us
  other arithmetic: 24 us -> 8.7 us
  between operations: 14.3 us -> 0.84 us
  local copies, waits for them, and re-layouts: 12.4 us -> 2.45 us
    psum x1 -> x0, waiting for transfers between devices: 98.7 us -> none  [device_step(): summed = lax.psum(packed, 'sp')]
    pallas_call x0 -> x2, Pallas kernels: none -> 60 us  [the longest x1 38.7 us: combine(): pl.pallas_call(functools.partial(combine_body, side, q_heads), out_shape=...]
    pmax x1 -> x0, blocking collectives: 51.5 us -> none  [device_step(): global_peak = lax.pmax(local_peak, 'sp')]
    dot_general x6 -> x3, matrix products: 61.1 us -> 28.8 us  [the longest x1 20.7 us: project_token(): jnp.dot(hidden, w_q, preferred_element_type=F32).astype(BF16)]
    select_n x1 -> x0, other arithmetic: 9.47 us -> none  [local_attention(): v_upd = jnp.where(write_mask, v_new[:, None], v_loc)]
    broadcast_in_dim x1 -> x0, local copies, waits for them, and re-layouts: 5.42 us -> none  [device_step(): (local_sum * factor)[..., None]]
    div x1 -> x0, local copies, waits for them, and re-layouts: 3.12 us -> none  [device_step(): summed[..., :head_dim] / summed[..., head_dim:]]
  transfers between devices with their start and end apart: 1 -> 0, of which waited for: 1 -> 0; matrix products, arithmetic and copies ran while one was open for 0% -> 0% of each run, Pallas kernels for 0% -> 0%
where the time goes in v1:
time: 101 us
  Pallas kernels  60 us (59%)
  matrix products  28.8 us (29%)
  other arithmetic  8.7 us (9%)
  local copies, waits for them, and re-layouts  2.45 us (2%)
    pallas_call x1, Pallas kernels, combine(): pl.pallas_call(functools.partial(combine_body, side, q_heads), out_shape=...  38.7 us
    pallas_call x1, Pallas kernels, attention(): pl.pallas_call(functools.partial(attn_body, seqs, slots, kv_heads, q_head...  21.4 us
    dot_general x1, matrix products, project_token(): jnp.dot(hidden, w_q, preferred_element_type=F32).astype(BF16)  20.7 us
    dot_general x1, matrix products, project_token(): jnp.dot(hidden, w_v, preferred_element_type=F32).astype(BF16)  6.12 us
    unnamed x14, local copies, waits for them, and re-layouts  2.3 us
    convert_element_type x3, other arithmetic, rms_scale(): gain.astype(F32)  2.1 us
    dot_general x1, matrix products, project_token(): jnp.dot(hidden, w_k, preferred_element_type=F32).astype(BF16)  2.02 us

profile of v1, /device:TPU:97, one launch (start us, length us, event | category | flops | bytes accessed | tf_op | source)
XLA Modules:
  0.0 100.9 jit_solution(8422463582073031376)
XLA Ops:
  0.6 0.0 copy-start
  0.6 0.7 convert_element_type.66
  1.4 0.7 convert_element_type.72
  2.0 0.7 convert_element_type.67
  2.7 0.0 slice-start
  2.7 1.5 %fusion.2 = f32[64]{0:T(128)S(1)} fusion(bf16[64,5120]{1,0:T(8,128)(2,1)} %tok_ref.1), kind=kLoop, calls=%fused_computation.5 | loop fusion | flops 982976 | bytes 655616 | tf_op jit(solution)/shard_map/reduce_sum | solution.py:19
  4.2 0.7 convert_element_type.61
  4.9 0.2 multiply_cosine_fusion
  5.1 0.0 copy-done
  5.1 0.0 slice-start.1
  5.1 0.0 slice-start.2
  5.1 6.1 %fusion.7 = bf16[8,8,8,128]{3,1,2,0:T(8,128)(2,1)S(1)} fusion(bf16[5120,1024]{1,0:T(8,128)(2,1)} %param.17, bf16[64,5120]{1,0:T(8,128)(2,1)S(1)} %copy-done, f32[5120]{0:T(1024)S(1)} %convert_element_type.61, f32[64]{0:T(128)S(1)} %add_rsqrt_fusion.2), kind=kOutput, calls=%fused_computation.16 | convolution fusion | flops 672464896 | bytes 11292928 | tf_op jit(solution)/shard_map/dot_general | solution.py:43
  11.3 0.0 slice-done
  11.3 0.0 slice-done.1
  11.3 0.0 slice-done.2
  11.3 2.0 %fusion.6 = f32[8,8,8,128]{3,1,2,0:T(8,128)S(1)} fusion(bf16[5120,1024]{1,0:T(8,128)(2,1)S(1)} %bitcast.37, bf16[64,5120]{1,0:T(8,128)(2,1)S(1)} %copy-done, f32[5120]{0:T(1024)S(1)} %convert_element_type.61, f32[64]{0:T(128)S(1)} %add_rsqrt_fusion.2), kind=kOutput, calls=%fused_computation.15 | convolution fusion | flops 672530432 | bytes 11424000 | tf_op jit(solution)/shard_map/dot_general | solution.py:42
  13.4 0.1 multiply_reduce_fusion.1
  13.6 0.1 copy.20
  13.6 0.1 copy.21
  13.7 0.1 multiply_multiply_fusion.1
  13.9 0.2 fusion.8
  14.0 0.1 pad_maximum_fusion
  14.2 0.0 copy-start.1
  14.2 0.9 bitcast_convert_fusion.kv_ref
  15.0 20.7 %fusion.1 = f32[8,8,40,128]{3,1,2,0:T(8,128)S(1)} fusion(bf16[5120,5120]{1,0:T(8,128)(2,1)} %param.15, bf16[64,5120]{1,0:T(8,128)(2,1)S(1)} %copy-done, f32[5120]{0:T(1024)S(1)} %convert_element_type.61, f32[64]{0:T(128)S(1)} %add_rsqrt_fusion.2), kind=kOutput, calls=%fused_computation.4 | convolution fusion | flops 3357409280 | bytes 54415616 | tf_op jit(solution)/shard_map/dot_general | solution.py:41
  35.7 0.0 copy-done.1
  35.7 0.2 copy.24
  36.0 0.4 multiply_reduce_fusion
  36.4 0.4 multiply_multiply_fusion
  36.8 0.6 subtract_convert_fusion
  37.4 1.4 %maximum_convert_fusion.q_ref = f32[2560,128]{1,0:T(8,128)} fusion(bf16[2560,64]{1,0:T(8,128)(2,1)S(1)} %bitcast.42, bf16[2560,64]{1,0:T(8,128)(2,1)S(1)} %bitcast.41), kind=kLoop, calls=%fused_computation.17 | loop fusion | flops 1310720 | bytes 1966080 | tf_op jit(solution)/shard_map/convert_element_type | solution.py:376
  38.8 21.4 %attend.1 = (bf16[64,32,16,128]{3,2,1,0:T(8,128)(2,1)}, bf16[64,32,16,128]{3,2,1,0:T(8,128)(2,1)}, f32[2560,128]{1,0:T(8,128)}, f32[8,2,8,128]{3,2,1,0:T(8,128)}) custom-call(s32[64]{0:T(128)} %pos_ref.1, s32[1]{0:T(128)} %bitcast.start_ref, f32[2560,128]{1,0:T(8,128)} %maximum_convert_fusion.q_ref, f32[1024,128]{1,0:T(8,128)} %bitcast_convert_fusion.kv_ref, ...), custom_call_target="tpu_custom_call" | custom-call | tf_op jit(solution)/shard_map/attend/pallas_call | solution.py:121
  60.2 38.7 %combine.1 = bf16[64,5120]{1,0:T(8,128)(2,1)} custom-call(f32[2,4,4,80,128]{4,3,2,1,0:T(8,128)} %bitcast.44, f32[2,4,2,8,128]{4,3,2,1,0:T(8,128)} %bitcast.46, bf16[64,5120]{1,0:T(8,128)(2,1)} %tok_ref.1, bf16[5120,5120]{1,0:T(8,128)(2,1)} %wo_ref.1), custom_call_target="tpu_custom_call" | custom-call | tf_op jit(solution)/shard_map/combine/pallas_call | solution.py:337
  98.9 2.0 %copy.28 = bf16[64,5120]{1,0:T(8,128)(2,1)} copy(bf16[64,5120]{1,0:T(8,128)(2,1)} %combine.1) | data formatting | bytes 1310720
  (7 shorter events, 0.1 us)
Async XLA Ops:
  0.6 4.5 %copy-start = (bf16[64,5120]{1,0:T(8,128)(2,1)S(1)}, bf16[64,5120]{1,0:T(8,128)(2,1)}, u32[]{:S(2)}) copy-start(bf16[64,5120]{1,0:T(8,128)(2,1)} %tok_ref.1) | copy-start | bytes 1966084
  2.7 8.6 %slice-start = ((s8[10485760]{0:T(1024)(128)(4,1)}), s8[4194304]{0:T(1024)(128)(4,1)S(1)}, s32[]{:S(2)}) async-start(s8[10485760]{0:T(1024)(128)(4,1)} %bitcast.36), calls=%async_computation | async-start | bytes 8388608
  5.1 6.2 %slice-start.1 = ((s8[10485760]{0:T(1024)(128)(4,1)}), s8[4194304]{0:T(1024)(128)(4,1)S(1)}, s32[]{:S(2)}) async-start(s8[10485760]{0:T(1024)(128)(4,1)} %bitcast.36), calls=%async_computation.1 | async-start | bytes 8388608
  5.1 6.2 %slice-start.2 = ((s8[10485760]{0:T(1024)(128)(4,1)}), s8[2097152]{0:T(1024)(128)(4,1)S(1)}, s32[]{:S(2)}) async-start(s8[10485760]{0:T(1024)(128)(4,1)} %bitcast.36), calls=%async_computation.2 | async-start | bytes 4194304
  14.2 21.6 %copy-start.1 = (bf16[64,2,8,128]{3,2,1,0:T(8,128)(2,1)}, bf16[64,2,8,128]{3,2,1,0:T(8,128)(2,1)S(1)}, u32[]{:S(2)}) copy-start(bf16[64,2,8,128]{3,2,1,0:T(8,128)(2,1)S(1)} %pad_maximum_fusion) | copy-start | bytes 786436

commit v2 on v1

--- a/solution.py
+++ b/solution.py
@@ -2,6 +2,7 @@
 
 import jax
 import jax.numpy as jnp
+import numpy as np
 from jax import lax
 from jax.experimental import pallas as pl
 from jax.experimental.pallas import tpu as pltpu
@@ -15,37 +16,133 @@
 BF16 = jnp.bfloat16
 
 
-def rms_scale(values, gain):
-    return values * lax.rsqrt(jnp.mean(values * values, axis=-1, keepdims=True) + NORM_EPS) * gain.astype(F32)
-
-
-def rope_table(positions, head_dim):
-    inv_freq = ROPE_THETA ** (-jnp.arange(head_dim // 2, dtype=F32) * 2.0 / head_dim)
-    angles = positions.astype(F32)[:, None] * inv_freq[None, :]
-    return jnp.cos(angles)[:, None, :], jnp.sin(angles)[:, None, :]
-
-
-def norm_rope(proj, gain, cos_table, sin_table):
-    normed = rms_scale(proj.astype(F32), gain)
-    half_dim = proj.shape[-1] // 2
-    first_half = normed[..., :half_dim]
-    second_half = normed[..., half_dim:]
-    rotated = jnp.concatenate([first_half * cos_table - second_half * sin_table, second_half * cos_table + first_half * sin_table], axis=-1)
-    return rotated.astype(BF16)
-
-
-def project_token(tokens, positions, w_q, w_k, w_v, attn_norm, q_norm, k_norm):
-    seq_count = tokens.shape[0]
+def project_body(seq_count, q_heads, kv_heads, head_dim, tok_ref, gain_ref, pos_ref, freq_ref, wq_ref, wk_ref, wv_ref,
+                 q_ref, kv_ref, hid, wbuf, stage, taken, w_sem, s_sem, r_sem):
+    me = lax.axis_index("sp")
+    core = lax.rem(me, 2)
+    partner = me + 1 - 2 * core
+    dim = tok_ref.shape[1]
+    chunks, _, width = wbuf.shape
+    per = width // head_dim
+    splits = w_sem.shape[1]
+    rows = dim // splits
+    kv_chunks = kv_heads // 2 // per
+    q_chunks = chunks - 2 * kv_chunks
+
+    def source(i):
+        if i < kv_chunks:
+            return wk_ref, core * (kv_heads // 2) + i * per
+        if i < 2 * kv_chunks:
+            return wv_ref, core * (kv_heads // 2) + (i - kv_chunks) * per
+        return wq_ref, core * (q_heads // 2) + (i - 2 * kv_chunks) * per
+
+    def fetch(i, j):
+        ref, head = source(i)
+        return pltpu.make_async_copy(
+            ref.at[pl.ds(j * rows, rows), pl.ds(pl.multiple_of(head * head_dim, 128), width)],
+            wbuf.at[i, pl.ds(j * rows, rows), :], w_sem.at[i, j])
+
+    pieces = [(i, j) for i in range(chunks) for j in range(splits)]
+    ahead = 5
+    for i, j in pieces[:ahead]:
+        fetch(i, j).start()
+
+    barrier = pltpu.get_barrier_semaphore()
+    pl.semaphore_signal(barrier, inc=1, device_id={"sp": partner}, device_id_type=MESH)
+
+    gain = gain_ref[:, :dim]
+    q_gain = gain_ref[:, dim:dim + head_dim]
+    k_gain = gain_ref[:, dim + head_dim:dim + 2 * head_dim]
+    tok = tok_ref[...].astype(F32)
+    hid[...] = (tok * lax.rsqrt(jnp.mean(tok * tok, axis=-1, keepdims=True) + NORM_EPS) * gain).astype(BF16)
+    eye = lax.broadcasted_iota(jnp.int32, (seq_count, seq_count), 0) == lax.broadcasted_iota(jnp.int32, (seq_count, seq_count), 1)
+    pos = jnp.sum(jnp.where(eye, pos_ref[...].astype(F32), 0.0), axis=1, keepdims=True)
+    angles = pos * freq_ref[...]
+    cos = jnp.cos(angles)
+    lower = lax.broadcasted_iota(jnp.int32, (seq_count, head_dim), 1) < head_dim // 2
+    sin = jnp.sin(angles)
+    sin = jnp.where(lower, -sin, sin)
+    pl.semaphore_wait(barrier, 1)
+
+    def place(i, side, buf):
+        for n in range(per):
+            value = buf[i, :, n * head_dim:(n + 1) * head_dim]
+            if i < 2 * kv_chunks:
+                head = side * (kv_heads // 2) + (i % kv_chunks) * per + n + (kv_heads if i >= kv_chunks else 0)
+                kv_ref[pl.ds(head, seq_count, stride=2 * kv_heads), :] = value
+            else:
+                head = side * (q_heads // 2) + (i - 2 * kv_chunks) * per + n
+                q_ref[pl.ds(head, seq_count, stride=q_heads), :] = value
+
+    swaps = []
+    for i in range(chunks):
+        acc = None
+        for j in range(splits):
+            at = i * splits + j
+            fetch(i, j).wait()
+            if at + ahead < len(pieces):
+                fetch(*pieces[at + ahead]).start()
+            part = jnp.dot(hid[:, j * rows:(j + 1) * rows], wbuf[i, j * rows:(j + 1) * rows, :], preferred_element_type=F32)
+            acc = part if acc is None else acc + part
+        acc = acc.astype(BF16).astype(F32)
+        for n in range(per):
+            value = acc[:, n * head_dim:(n + 1) * head_dim]
+            if not kv_chunks <= i < 2 * kv_chunks:
+                scale = lax.rsqrt(jnp.mean(value * value, axis=-1, keepdims=True) + NORM_EPS)
+                value = value * scale * (k_gain if i < kv_chunks else q_gain)
+                value = value * cos + pltpu.roll(value, head_dim // 2, 1) * sin
+                value = value.astype(BF16).astype(F32)
+            stage[i, :, n * head_dim:(n + 1) * head_dim] = value
+        copy = pltpu.make_async_remote_copy(
+            src_ref=stage.at[i], dst_ref=taken.at[i], send_sem=s_sem.at[i], recv_sem=r_sem.at[i],
+            device_id={"sp": partner}, device_id_type=MESH)
+        copy.start()
+        swaps.append(copy)
+        place(i, core, stage)
+        if i > 0:
+            swaps[i - 1].wait_recv()
+            place(i - 1, 1 - core, taken)
+    swaps[-1].wait_recv()
+    place(chunks - 1, 1 - core, taken)
+    for copy in swaps:
+        copy.wait_send()
+
+
+def project(tokens, positions, w_q, w_k, w_v, attn_norm, q_norm, k_norm):
+    seq_count, dim = tokens.shape
     head_dim = q_norm.shape[0]
-    hidden = rms_scale(tokens.astype(F32), attn_norm).astype(BF16)
-    q_proj = jnp.dot(hidden, w_q, preferred_element_type=F32).astype(BF16).reshape(seq_count, -1, head_dim)
-    k_proj = jnp.dot(hidden, w_k, preferred_element_type=F32).astype(BF16).reshape(seq_count, -1, head_dim)
-    v_new = jnp.dot(hidden, w_v, preferred_element_type=F32).astype(BF16).reshape(seq_count, -1, head_dim)
-    cos_table, sin_table = rope_table(positions, head_dim)
-    return norm_rope(q_proj, q_norm, cos_table, sin_table), norm_rope(k_proj, k_norm, cos_table, sin_table), v_new
-
-
-def attn_body(seqs, slots, kv_heads, q_heads, pos_ref, start_ref, q_ref, kv_ref, k_ref, v_ref, ko_ref, vo_ref, o_ref, ml_ref):
+    q_heads = w_q.shape[1] // head_dim
+    kv_heads = w_k.shape[1] // head_dim
+    width = 4 * head_dim
+    chunks = (w_q.shape[1] + w_k.shape[1] + w_v.shape[1]) // 2 // width
+    splits = 2
+    gains = jnp.concatenate([attn_norm, q_norm, k_norm]).astype(F32).reshape(1, -1)
+    half = ROPE_THETA ** (-np.arange(head_dim // 2, dtype=np.float64) * 2.0 / head_dim)
+    freq = jnp.asarray(np.concatenate([half, half]).astype(np.float32)).reshape(1, head_dim)
+    vmem = pl.BlockSpec(memory_space=pltpu.VMEM)
+    hbm = pl.BlockSpec(memory_space=pl.ANY)
+    dma = pltpu.SemaphoreType.DMA
+    return pl.pallas_call(
+        functools.partial(project_body, seq_count, q_heads, kv_heads, head_dim),
+        out_shape=[
+            jax.ShapeDtypeStruct((seq_count * q_heads, head_dim), F32),
+            jax.ShapeDtypeStruct((seq_count * 2 * kv_heads, head_dim), F32),
+        ],
+        in_specs=[vmem, vmem, vmem, vmem, hbm, hbm, hbm],
+        out_specs=[vmem, vmem],
+        scratch_shapes=[
+            pltpu.VMEM((seq_count, dim), BF16),
+            pltpu.VMEM((chunks, dim, width), BF16),
+            pltpu.VMEM((chunks, seq_count, width), F32),
+            pltpu.VMEM((chunks, seq_count, width), F32),
+            dma((chunks, splits)), dma((chunks,)), dma((chunks,)),
+        ],
+        compiler_params=pltpu.CompilerParams(collective_id=0, has_side_effects=True, vmem_limit_bytes=60 * 1024 * 1024),
+        name="project",
+    )(tokens, gains, positions.reshape(1, -1), freq, w_q, w_k, w_v)
+
+
+def attn_body(seqs, slots, kv_heads, q_heads, pos_ref, start_ref, q_ref, kv_ref, k_ref, v_ref, ko_ref, vo_ref, o_ref, ml_ref, sc_ref, pw_ref):
     head_dim = q_ref.shape[-1]
     step = pl.program_id(0)
     scale = head_dim ** -0.5
@@ -77,20 +174,28 @@
             ko_ref[b, tile] = jnp.where(hit, k_two, ko_ref[b, tile].astype(F32)).astype(BF16)
             vo_ref[b, tile] = jnp.where(hit, v_two, vo_ref[b, tile].astype(F32)).astype(BF16)
 
+    peaks = []
     for b in range(seqs):
         rel = pos_ref[step * seqs + b] - start_ref[0]
         keys = ko_ref[b].reshape(cols, head_dim)
-        vals = vo_ref[b].reshape(cols, head_dim)
         query = q_ref[pl.ds(b * q_heads, q_heads), :].astype(BF16)
         scores = lax.dot_general(query, keys, (((1,), (1,)), ((), ())), preferred_element_type=F32) * scale
-        live = slot_of <= rel
-        scores = jnp.where(live, scores, NEG_FILL)
-        peak = jnp.max(scores, axis=1, keepdims=True)
-        weights = jnp.where(live, jnp.exp(scores - peak), 0.0)
-        total = jnp.sum(weights, axis=1, keepdims=True)
-        o_ref[pl.ds(b * q_heads, q_heads), :] = jnp.dot(weights.astype(BF16), vals, preferred_element_type=F32)
+        scores = jnp.where(slot_of <= rel, scores, -jnp.inf)
+        sc_ref[b] = scores
+        peaks.append(jnp.max(scores, axis=1, keepdims=True))
+    totals = []
+    for b in range(seqs):
+        rel = pos_ref[step * seqs + b] - start_ref[0]
+        shift = jnp.where(rel < 0, 0.0, peaks[b])
+        weights = jnp.exp(sc_ref[b] - shift)
+        totals.append(jnp.sum(weights, axis=1, keepdims=True))
+        pw_ref[b] = weights.astype(BF16)
+    for b in range(seqs):
+        vals = vo_ref[b].reshape(cols, head_dim)
+        o_ref[pl.ds(b * q_heads, q_heads), :] = jnp.dot(pw_ref[b], vals, preferred_element_type=F32)
+        peak = jnp.maximum(peaks[b], NEG_FILL)
         ml_ref[0, 0, pl.ds(b, 1), :] = jnp.sum(jnp.where(diag, peak, 0.0), axis=0, keepdims=True)
-        ml_ref[0, 1, pl.ds(b, 1), :] = jnp.sum(jnp.where(diag, total, 0.0), axis=0, keepdims=True)
+        ml_ref[0, 1, pl.ds(b, 1), :] = jnp.sum(jnp.where(diag, totals[b], 0.0), axis=0, keepdims=True)
 
 
 def attention(q_rows, kv_rows, positions, shard_start, k_cache, v_cache):
@@ -117,6 +222,10 @@
             pl.BlockSpec((seqs * q_heads, head_dim), lambda i, *_: (i, 0)),
             pl.BlockSpec((1, 2, seqs, head_dim), lambda i, *_: (i, 0, 0, 0)),
         ],
+        scratch_shapes=[
+            pltpu.VMEM((seqs, q_heads, slots * kv_heads), F32),
+            pltpu.VMEM((seqs, q_heads, slots * kv_heads), BF16),
+        ],
     )
     k_out, v_out, part, ml = pl.pallas_call(
         functools.partial(attn_body, seqs, slots, kv_heads, q_heads),
@@ -148,8 +257,8 @@
     return jnp.transpose(tile)
 
 
-def combine_body(side, q_heads, o_ref, ml_ref, tok_ref, wo_ref, out_ref,
-                 r1, rm1, s1, sm1, r2, rm2, s2, sm2, r3, rm3, obuf, lhs, wbuf, gbuf, acc,
+def combine_body(side, q_heads, o_ref, ml_ref, wo_ref, out_ref,
+                 r1, rm1, s1, sm1, r2, rm2, s2, sm2, r3, rm3, obuf, lhs, wbuf, gbuf,
                  w_sem, a_s, a_r, b_s, b_r, c_s, c_r, d_s, d_r, e_s, e_r, f_s, f_r, h_s, h_r):
     me = lax.axis_index("sp")
     core = lax.rem(me, 2)
@@ -308,8 +417,7 @@
         g3[key].wait_recv()
     for half in range(2):
         for p in range(2 * side * side):
-            acc[2 * p:2 * p + 2, half * width:(half + 1) * width] = gbuf[half, p]
-    out_ref[...] = (tok_ref[...].astype(F32) + acc[...]).astype(BF16)
+            out_ref[2 * p:2 * p + 2, half * width:(half + 1) * width] = gbuf[half, p]
 
     for group in (in1, in2, in3):
         for pair in group.values():
@@ -336,8 +444,8 @@
     stat = (side, 2, ml.shape[2], head_dim)
     return pl.pallas_call(
         functools.partial(combine_body, side, q_heads),
-        out_shape=jax.ShapeDtypeStruct(tokens.shape, BF16),
-        in_specs=[vmem, vmem, vmem, pl.BlockSpec(memory_space=pl.ANY)],
+        out_shape=jax.ShapeDtypeStruct(tokens.shape, F32),
+        in_specs=[vmem, vmem, pl.BlockSpec(memory_space=pl.ANY)],
         out_specs=vmem,
         scratch_shapes=[
             pltpu.VMEM(piece, F32), pltpu.VMEM(stat, F32),
@@ -349,7 +457,6 @@
             pltpu.VMEM((8, depth), F32),
             pltpu.VMEM((depth, width), BF16),
             pltpu.VMEM((2, 2 * side * side, 2, width), F32),
-            pltpu.VMEM(tokens.shape, F32),
             dma((4,)),
             dma((side, 2)), dma((side, 2)),
             dma((side, 2)), dma((side, 2)),
@@ -361,7 +468,7 @@
         ],
         compiler_params=pltpu.CompilerParams(collective_id=1, has_side_effects=True, vmem_limit_bytes=60 * 1024 * 1024),
         name="combine",
-    )(o5, m5, tokens, w_o)
+    )(o5, m5, w_o)
 
 
 def solution(mesh):
@@ -369,14 +476,13 @@
     side = int(round((mesh.shape['sp'] // 2) ** 0.5))
 
     def device_step(tokens, positions, k_cache, v_cache, w_q, w_k, w_v, w_o, attn_norm, q_norm, k_norm):
-        q_rot, k_rot, v_new = project_token(tokens, positions, w_q, w_k, w_v, attn_norm, q_norm, k_norm)
-        head_dim = q_norm.shape[0]
-        new_kv = jnp.stack([k_rot, v_new], axis=1)
-        shard_start = (lax.axis_index('sp') * k_cache.shape[1]).astype(jnp.int32).reshape(1)
-        q_rows = q_rot.astype(F32).reshape(-1, head_dim)
-        kv_rows = new_kv.astype(F32).reshape(-1, head_dim)
+        seq_count, slots, kv_heads, head_dim = k_cache.shape
+        shard_start = (lax.axis_index('sp') * slots).astype(jnp.int32).reshape(1)
+        q_rows, kv_rows = project(tokens, positions, w_q, w_k, w_v, attn_norm, q_norm, k_norm)
+        new_kv = kv_rows.astype(BF16).reshape(seq_count, 2, kv_heads, head_dim)
         k_upd, v_upd, part, ml = attention(q_rows, kv_rows, positions, shard_start, k_cache, v_cache)
-        block_out = combine(part, ml, tokens, w_o, side)
+        mixed = combine(part, ml, tokens, w_o, side)
+        block_out = (tokens.astype(F32) + mixed).astype(BF16)
         return block_out, k_upd, v_upd, new_kv
 
     return jax.shard_map(device_step, mesh=mesh, in_specs=(P('dp', None), P('dp'), cache_spec, cache_spec, P(), P(), P(), P(), P(), P(), P()), out_specs=(P('dp', None), cache_spec, cache_spec, P('dp', None, None, None)), check_vma=False)

time: 101 us -> 78.5 us (0.78)
  matrix products: 28.8 us -> 0 us
  Pallas kernels: 60 us -> 72.4 us
  other arithmetic: 8.7 us -> 4.3 us
  local copies, waits for them, and re-layouts: 2.45 us -> 0.72 us
    dot_general x3 -> x0, matrix products: 28.8 us -> none  [the longest x1 20.7 us: project_token(): jnp.dot(hidden, w_q, preferred_element_type=F32).astype(BF16)]
    pallas_call x0 -> x1, Pallas kernels: none -> 18.6 us  [project(): pl.pallas_call(functools.partial(project_body, seq_count, q_heads, kv_hea...]
    pallas_call x1, Pallas kernels: 21.4 us -> 17.1 us  [attention(): pl.pallas_call(functools.partial(attn_body, seqs, slots, kv_heads, q_head...]
    unnamed x14 -> x4, local copies, waits for them, and re-layouts: 2.3 us -> 0.01 us
    reduce_sum x3 -> x0, other arithmetic: 2.01 us -> none  [rms_scale(): jnp.mean(values * values, axis=-1, keepdims=True) + NORM_EPS]
    pallas_call x1, Pallas kernels: 38.7 us -> 36.8 us  [combine(): pl.pallas_call(functools.partial(combine_body, side, q_heads), out_shape=...]
    convert_element_type x6 -> x3, other arithmetic: 5.02 us -> 4.3 us  [the longest x1 2.26 us: device_step(): block_out = (tokens.astype(F32) + mixed).astype(BF16)]
where the time goes in v2:
time: 78.5 us; the launch traced here: 78.1 us
  Pallas kernels  72.4 us (92%)
  other arithmetic  4.3 us (5%)
    pallas_call x1, Pallas kernels, combine(): pl.pallas_call(functools.partial(combine_body, side, q_heads), out_shape=...  36.8 us
    pallas_call x1, Pallas kernels, project(): pl.pallas_call(functools.partial(project_body, seq_count, q_heads, kv_hea...  18.6 us
    pallas_call x1, Pallas kernels, attention(): pl.pallas_call(functools.partial(attn_body, seqs, slots, kv_heads, q_head...  17.1 us
    convert_element_type x1, other arithmetic, device_step(): block_out = (tokens.astype(F32) + mixed).astype(BF16)  2.26 us

profile of v2, /device:TPU:97, one launch (start us, length us, event | category | flops | bytes accessed | tf_op | source)
XLA Modules:
  0.0 78.1 jit_solution(17781880553860109888)
XLA Ops:
  0.6 0.7 concatenate.16
  1.3 1.3 %maximum_convert_fusion.gain_ref = f32[1,5376]{1,0:T(1,128)} fusion(bf16[1,128]{1,0:T(2,128)(2,1)} %bitcast.17, bf16[1,128]{1,0:T(2,128)(2,1)} %bitcast.18, bf16[1,5120]{1,0:T(2,128)(2,1)S(1)} %concatenate.16), kind=kLoop, calls=%fused_computation.1 | loop fusion | flops 32256 | bytes 32256 | tf_op jit(solution)/shard_map/convert_element_type | solution.py:119
  2.7 18.6 %project.1 = (f32[2560,128]{1,0:T(8,128)}, f32[1024,128]{1,0:T(8,128)}) custom-call(bf16[64,5120]{1,0:T(8,128)(2,1)} %tok_ref.1, f32[1,5376]{1,0:T(1,128)} %maximum_convert_fusion.gain_ref, s32[1,64]{1,0:T(1,128)} %bitcast.16, f32[1,128]{1,0:T(1,128)} %constant.9.freq_ref, bf16[5120,5120]{1,0:T(8,128)(2,1)} %wq_ref.1, bf16[5120,1024]{1,0:T(8,128)(2,1)} %wk_ref.1, ...), custom_call_target="tpu_custom_call" | custom-call | tf_op jit(solution)/shard_map/project/pallas_call | solution.py:125
  21.3 17.1 %attend.1 = (bf16[64,32,16,128]{3,2,1,0:T(8,128)(2,1)}, bf16[64,32,16,128]{3,2,1,0:T(8,128)(2,1)}, f32[2560,128]{1,0:T(8,128)}, f32[8,2,8,128]{3,2,1,0:T(8,128)}) custom-call(s32[64]{0:T(128)} %pos_ref.1, s32[1]{0:T(128)} %bitcast.start_ref, f32[2560,128]{1,0:T(8,128)} %get-tuple-element.10.q_ref, f32[1024,128]{1,0:T(8,128)} %get-tuple-element.11.kv_ref, ...), custom_call_target="tpu_custom_call" | custom-call | tf_op jit(solution)/shard_map/attend/pallas_call | solution.py:230
  38.4 0.0 copy-start
  38.4 0.0 copy-start.1
  38.4 36.8 %combine.1 = f32[64,5120]{1,0:T(8,128)} custom-call(f32[2,4,4,80,128]{4,3,2,1,0:T(8,128)} %bitcast.13, f32[2,4,2,8,128]{4,3,2,1,0:T(8,128)} %bitcast.15, bf16[5120,5120]{1,0:T(8,128)(2,1)} %wo_ref.1), custom_call_target="tpu_custom_call" | custom-call | tf_op jit(solution)/shard_map/combine/pallas_call | solution.py:445
  75.1 0.0 copy-done
  75.1 2.3 %add_convert_fusion = bf16[64,5120]{1,0:T(8,128)(2,1)} fusion(f32[64,5120]{1,0:T(8,128)} %combine.1, bf16[64,5120]{1,0:T(8,128)(2,1)S(1)} %copy-done), kind=kLoop, calls=%fused_computation | loop fusion | flops 983040 | bytes 2621440 | tf_op jit(solution)/shard_map/convert_element_type | solution.py:485
  77.4 0.0 copy-done.1
  77.4 0.7 convert_element_type.22
Async XLA Ops:
  38.4 36.8 %copy-start = (bf16[64,5120]{1,0:T(8,128)(2,1)S(1)}, bf16[64,5120]{1,0:T(8,128)(2,1)}, u32[]{:S(2)}) copy-start(bf16[64,5120]{1,0:T(8,128)(2,1)} %tok_ref.1) | copy-start | bytes 1966084
  38.4 39.0 %copy-start.1 = (f32[1024,128]{1,0:T(8,128)S(1)}, f32[1024,128]{1,0:T(8,128)}, u32[]{:S(2)}) copy-start(f32[1024,128]{1,0:T(8,128)} %get-tuple-element.11.kv_ref) | copy-start | bytes 1572868

commit v3 on v0

v3 whole, which is shorter than its diff:
```python
import functools

import jax
import jax.numpy as jnp
import numpy as np
from jax import lax
from jax.experimental import pallas as pl
from jax.experimental.pallas import tpu as pltpu
from jax.sharding import PartitionSpec as P

NORM_EPS = 1e-6
ROPE_THETA = 1000000.0
NEG_FILL = -1e30
MESH = pl.DeviceIdType.MESH
F32 = jnp.float32
BF16 = jnp.bfloat16
MIB = 1024 * 1024
LIMIT_A = 27 * MIB
LIMIT_B = 28 * MIB
LIMIT_C = 37 * MIB


def project_body(seq_count, q_heads, kv_heads, head_dim, tok_ref, gain_ref, qn_ref, kn_ref, pos_ref, freq_ref, wq_ref, wk_ref, wv_ref,
                 heads, tok, hid, wbuf, w_sem, t_sem, s_sem, r_sem):
    me = lax.axis_index("sp")
    core = lax.rem(me, 2)
    partner = me + 1 - 2 * core
    dim = tok_ref.shape[1]
    slots, _, width = wbuf.shape
    chunks = w_sem.shape[0]
    per = width // head_dim
    splits = w_sem.shape[1]
    rows = dim // splits
    kv_chunks = kv_heads // 2 // per

    def first_head(i, side):
        if i < kv_chunks:
            return side * (kv_heads // 2) + i * per, wk_ref, side * (kv_heads // 2) + i * per
        if i < 2 * kv_chunks:
            own = side * (kv_heads // 2) + (i - kv_chunks) * per
            return kv_heads + own, wv_ref, own
        own = side * (q_heads // 2) + (i - 2 * kv_chunks) * per
        return 2 * kv_heads + own, wq_ref, own

    def fetch(i, j):
        _, ref, head = first_head(i, core)
        return pltpu.make_async_copy(
            ref.at[pl.ds(j * rows, rows), pl.ds(pl.multiple_of(head * head_dim, 128), width)],
            wbuf.at[i % slots, pl.ds(j * rows, rows), :], w_sem.at[i, j])

    load = pltpu.make_async_copy(tok_ref, tok, t_sem)
    load.start()
    pieces = [(i, j) for i in range(chunks) for j in range(splits)]
    ahead = 3
    for i, j in pieces[:ahead]:
        fetch(i, j).start()

    barrier = pltpu.get_barrier_semaphore()
    pl.semaphore_signal(barrier, inc=1, device_id={"sp": partner}, device_id_type=MESH)

    eye = lax.broadcasted_iota(jnp.int32, (seq_count, seq_count), 0) == lax.broadcasted_iota(jnp.int32, (seq_count, seq_count), 1)
    pos = jnp.sum(jnp.where(eye, pos_ref[...].astype(F32), 0.0), axis=1, keepdims=True)
    angles = pos * freq_ref[...]
    cos = jnp.cos(angles)
    lower = lax.broadcasted_iota(jnp.int32, (seq_count, head_dim), 1) < head_dim // 2
    sin = jnp.sin(angles)
    sin = jnp.where(lower, -sin, sin)
    q_gain = qn_ref[...].astype(F32)
    k_gain = kn_ref[...].astype(F32)
    load.wait()
    values = tok[...].astype(F32)
    scale = lax.rsqrt(jnp.mean(values * values, axis=-1, keepdims=True) + NORM_EPS)
    for j in range(dim // 128):
        at = slice(j * 128, (j + 1) * 128)
        hid[:, at] = (tok[:, at].astype(F32) * scale * gain_ref[j:j + 1, :].astype(F32)).astype(BF16)
    pl.semaphore_wait(barrier, 1)

    swaps = []
    blocks, _, block, _ = heads.shape
    for i in range(chunks):
        acc = None
        for j in range(splits):
            at = i * splits + j
            fetch(i, j).wait()
            if at + ahead < len(pieces):
                fetch(*pieces[at + ahead]).start()
            part = jnp.dot(hid[:, j * rows:(j + 1) * rows], wbuf[i % slots, j * rows:(j + 1) * rows, :], preferred_element_type=F32)
            acc = part if acc is None else acc + part
        acc = acc.astype(BF16).astype(F32)
        at = first_head(i, core)[0]
        for n in range(per):
            value = acc[:, n * head_dim:(n + 1) * head_dim]
            if not kv_chunks <= i < 2 * kv_chunks:
                scale = lax.rsqrt(jnp.mean(value * value, axis=-1, keepdims=True) + NORM_EPS)
                value = value * scale * (k_gain if i < kv_chunks else q_gain)
                value = value * cos + pltpu.roll(value, head_dim // 2, 1) * sin
                value = value.astype(BF16).astype(F32)
            for m in range(blocks):
                heads[m, at + n] = value[m * block:(m + 1) * block]
        span = heads.at[:, pl.ds(at, per)]
        copy = pltpu.make_async_remote_copy(
            src_ref=span, dst_ref=span, send_sem=s_sem.at[i], recv_sem=r_sem.at[i],
            device_id={"sp": partner}, device_id_type=MESH)
        copy.start()
        swaps.append(copy)
    for copy in swaps:
        copy.wait()


def project(seqs, tokens, positions, w_q, w_k, w_v, attn_norm, q_norm, k_norm):
    seq_count, dim = tokens.shape
    head_dim = q_norm.shape[0]
    q_heads = w_q.shape[1] // head_dim
    kv_heads = w_k.shape[1] // head_dim
    width = 4 * head_dim
    chunks = (w_q.shape[1] + w_k.shape[1] + w_v.shape[1]) // 2 // width
    splits = 2
    half = ROPE_THETA ** (-np.arange(head_dim // 2, dtype=np.float64) * 2.0 / head_dim)
    freq = jnp.asarray(np.concatenate([half, half]).astype(np.float32)).reshape(1, head_dim)
    vmem = pl.BlockSpec(memory_space=pltpu.VMEM)
    hbm = pl.BlockSpec(memory_space=pl.ANY)
    dma = pltpu.SemaphoreType.DMA
    return pl.pallas_call(
        functools.partial(project_body, seq_count, q_heads, kv_heads, head_dim),
        out_shape=jax.ShapeDtypeStruct((seq_count // seqs, q_heads + 2 * kv_heads, seqs, head_dim), F32),
        in_specs=[hbm, vmem, vmem, vmem, vmem, vmem, hbm, hbm, hbm],
        out_specs=vmem,
        scratch_shapes=[
            pltpu.VMEM((seq_count, dim), BF16),
            pltpu.VMEM((seq_count, dim), BF16),
            pltpu.VMEM((4, dim, width), BF16),
            dma((chunks, splits)), dma, dma((chunks,)), dma((chunks,)),
        ],
        compiler_params=pltpu.CompilerParams(collective_id=0, has_side_effects=True, vmem_limit_bytes=LIMIT_A),
        name="project",
    )(*[pltpu.with_memory_space_constraint(a, pltpu.HBM) for a in (
        tokens, attn_norm.reshape(-1, 128), q_norm.reshape(1, -1), k_norm.reshape(1, -1), positions.reshape(1, -1), freq, w_q, w_k, w_v)])


def attn_body(steps, seqs, slots, kv_heads, q_heads, pos_ref, start_ref, heads, k_ref, v_ref, ko_ref, vo_ref, obuf, nk_ref,
              kbuf, vbuf, nkbuf, sc_ref, pw_ref, o_sem):
    head_dim = k_ref.shape[-1]
    scale = head_dim ** -0.5
    cols = slots * kv_heads
    group = q_heads // kv_heads
    o_rows = seqs * q_heads

    def span(i):
        return pl.ds(i * seqs, seqs)

    def caches_out(i):
        slot = lax.rem(i, 2)
        return [
            pltpu.make_async_copy(kbuf.at[slot], ko_ref.at[span(i)], o_sem.at[i, 2]),
            pltpu.make_async_copy(vbuf.at[slot], vo_ref.at[span(i)], o_sem.at[i, 3]),
        ]

    def rest_out(i):
        return [
            pltpu.make_async_copy(nkbuf.at[span(i)], nk_ref.at[span(i)], o_sem.at[i, 1]),
        ]

    row_id = lax.broadcasted_iota(jnp.int32, (q_heads, cols), 0)
    col_id = lax.broadcasted_iota(jnp.int32, (q_heads, cols), 1)
    own_head = jnp.zeros((q_heads, cols), jnp.int32)
    for h in range(1, kv_heads):
        own_head += (row_id >= h * group).astype(jnp.int32)
    slot_of = jnp.where(lax.rem(col_id, kv_heads) == own_head, lax.div(col_id, kv_heads), 1 << 20)
    upper = lax.broadcasted_iota(jnp.int32, (2 * kv_heads, head_dim), 0) >= kv_heads
    diag_r = lax.broadcasted_iota(jnp.int32, (q_heads, head_dim), 0)
    diag_c = lax.broadcasted_iota(jnp.int32, (q_heads, head_dim), 1)
    diag = diag_r == diag_c

    @pl.loop(0, steps)
    def _(i):
        rows_of = heads.at[i].reshape((2 * kv_heads + q_heads) * seqs, head_dim)
        slot = lax.rem(i, 2)

        @pl.when(i >= 2)
        def _():
            for copy in caches_out(i - 2):
                copy.wait()

        for b in range(seqs):
            rel = pos_ref[i * seqs + b] - start_ref[0]
            at = i * seqs + b
            kbuf[slot, b] = k_ref[at]
            vbuf[slot, b] = v_ref[at]
            k_new = rows_of[pl.ds(b, kv_heads, stride=seqs), :]
            v_new = rows_of[pl.ds(b + kv_heads * seqs, kv_heads, stride=seqs), :]
            nkbuf[at] = jnp.concatenate([k_new, v_new], axis=0).astype(BF16)

            @pl.when((rel >= 0) & (rel < slots))
            def _():
                tile = lax.div(rel, 2)
                hit = upper == (lax.rem(rel, 2) == 1)
                k_two = jnp.concatenate([k_new, k_new], axis=0)
                v_two = jnp.concatenate([v_new, v_new], axis=0)
                kbuf[slot, b, tile] = jnp.where(hit, k_two, kbuf[slot, b, tile].astype(F32)).astype(BF16)
                vbuf[slot, b, tile] = jnp.where(hit, v_two, vbuf[slot, b, tile].astype(F32)).astype(BF16)
        for copy in caches_out(i):
            copy.start()
        peaks = []
        for b in range(seqs):
            rel = pos_ref[i * seqs + b] - start_ref[0]
            keys = kbuf[slot, b].reshape(cols, head_dim)
            query = rows_of[pl.ds(b + 2 * kv_heads * seqs, q_heads, stride=seqs), :].astype(BF16)
            scores = lax.dot_general(query, keys, (((1,), (1,)), ((), ())), preferred_element_type=F32) * scale
            scores = jnp.where(slot_of <= rel, scores, -jnp.inf)
            sc_ref[b] = scores
            peaks.append(jnp.max(scores, axis=1, keepdims=True))
        totals = []
        for b in range(seqs):
            rel = pos_ref[i * seqs + b] - start_ref[0]
            shift = jnp.where(rel < 0, 0.0, peaks[b])
            weights = jnp.exp(sc_ref[b] - shift)
            totals.append(jnp.sum(weights, axis=1, keepdims=True))
            pw_ref[b] = weights.astype(BF16)
        for b in range(seqs):
            vals = vbuf[slot, b].reshape(cols, head_dim)
            obuf[i, pl.ds(b * q_heads, q_heads), :] = jnp.dot(pw_ref[b], vals, preferred_element_type=F32)
            peak = jnp.maximum(peaks[b], NEG_FILL)
            obuf[i, pl.ds(o_rows + b, 1), :] = jnp.sum(jnp.where(diag, peak, 0.0), axis=0, keepdims=True)
            obuf[i, pl.ds(o_rows + seqs + b, 1), :] = jnp.sum(jnp.where(diag, totals[b], 0.0), axis=0, keepdims=True)
        for copy in rest_out(i):
            copy.start()

    for i in range(steps):
        for copy in rest_out(i) + (caches_out(i) if i >= steps - 2 else []):
            copy.wait()


def attention(seqs, heads, positions, shard_start, k_cache, v_cache):
    seq_count, slots, kv_heads, head_dim = k_cache.shape
    q_heads = heads.shape[1] - 2 * kv_heads
    steps = seq_count // seqs
    pairs = slots // 2
    part_rows = seqs * q_heads + 2 * seqs
    k4 = k_cache.reshape(seq_count, pairs, 2 * kv_heads, head_dim)
    v4 = v_cache.reshape(seq_count, pairs, 2 * kv_heads, head_dim)
    hbm = pl.BlockSpec(memory_space=pl.ANY)
    vmem = pl.BlockSpec(memory_space=pltpu.VMEM)
    smem = pl.BlockSpec(memory_space=pltpu.SMEM)
    dma = pltpu.SemaphoreType.DMA
    k_out, v_out, part, new_kv = pl.pallas_call(
        functools.partial(attn_body, steps, seqs, slots, kv_heads, q_heads),
        in_specs=[smem, smem, vmem, vmem, vmem],
        out_specs=[hbm, hbm, vmem, hbm],
        out_shape=[
            jax.ShapeDtypeStruct(k4.shape, BF16),
            jax.ShapeDtypeStruct(v4.shape, BF16),
            jax.ShapeDtypeStruct((steps, part_rows, head_dim), F32),
            jax.ShapeDtypeStruct((seq_count, 2 * kv_heads, head_dim), BF16),
        ],
        scratch_shapes=[
            pltpu.VMEM((2, seqs) + k4.shape[1:], BF16),
            pltpu.VMEM((2, seqs) + v4.shape[1:], BF16),
            pltpu.VMEM((seq_count, 2 * kv_heads, head_dim), BF16),
            pltpu.VMEM((seqs, q_heads, slots * kv_heads), F32),
            pltpu.VMEM((seqs, q_heads, slots * kv_heads), BF16),
            dma((steps, 4)),
        ],
        compiler_params=pltpu.CompilerParams(vmem_limit_bytes=LIMIT_B),
        name="attend",
    )(positions, shard_start, heads, k4, v4)
    return (k_out.reshape(k_cache.shape), v_out.reshape(v_cache.shape), part,
            new_kv.reshape(seq_count, 2, kv_heads, head_dim))


def blend(stats):
    peak = stats[0][0]
    for m, _ in stats[1:]:
        peak = jnp.maximum(peak, m)
    factors = [jnp.exp(m - peak) for m, _ in stats]
    total = factors[0] * stats[0][1]
    for f, (_, l) in zip(factors[1:], stats[1:]):
        total += f * l
    return peak, total, factors


def combine_body(side, q_heads, seqs, o_ref, wo_ref, out_ref, r1, s1, r2, s2, r3, fin, obuf, lhs, wbuf, gbuf,
                 w_sem, a_s, a_r, b_s, b_r, c_s, c_r, d_s, d_r, e_s, e_r, f_s, f_r, h_s, h_r):
    me = lax.axis_index("sp")
    core = lax.rem(me, 2)
    chip = lax.div(me, 2)
    x = lax.rem(chip, side)
    y = lax.div(chip, side)
    first = x * (1 - core) + y * core
    second = y * (1 - core) + x * core
    stride1 = 2 * (1 - core) + 2 * side * core
    stride2 = 2 * side * (1 - core) + 2 * core
    partner = me + 1 - 2 * core
    head_dim = o_ref.shape[-1]
    depth, width = wbuf.shape
    w_parts = w_sem.shape[0]
    w_rows = depth // w_parts
    rows = 2 * q_heads
    body = side * rows
    stat_m, stat_l = pl.ds(body, seqs), pl.ds(body + seqs, seqs)
    order = [side // 2] + [d for d in range(1, side) if d != side // 2]

    def peer1(d):
        return me + (lax.rem(first + d, side) - first) * stride1

    def peer2(d):
        return me + (lax.rem(second + d, side) - second) * stride2

    def send(src, dst, ssem, rsem, to):
        copy = pltpu.make_async_remote_copy(src_ref=src, dst_ref=dst, send_sem=ssem, recv_sem=rsem, device_id={"sp": to}, device_id_type=MESH)
        copy.start()
        return copy

    barrier = pltpu.get_barrier_semaphore()
    neighbours = [partner] + [peer1(d) for d in range(1, side)] + [peer2(d) for d in range(1, side)]
    for n in neighbours:
        pl.semaphore_signal(barrier, inc=1, device_id={"sp": n}, device_id_type=MESH)
    pl.semaphore_wait(barrier, len(neighbours))

    in1 = {}
    for d in order + [0]:
        in1[d] = send(o_ref.at[1 - core, lax.rem(second + d, side)], r1.at[d], a_s.at[d], a_r.at[d], partner)
    w_copies = []
    for i in range(w_parts):
        copy = pltpu.make_async_copy(
            wo_ref.at[pl.ds(i * w_rows, w_rows), pl.ds(pl.multiple_of(core * width, 128), width)],
            wbuf.at[pl.ds(i * w_rows, w_rows), :], w_sem.at[i])
        copy.start()
        w_copies.append(copy)
    in2 = {}
    for d in order + [0]:
        in1[d].wait_recv()
        piece = lax.rem(first + d, side)
        peak, total, fac = blend([(o_ref[core, piece, stat_m, :], o_ref[core, piece, stat_l, :]), (r1[d, stat_m, :], r1[d, stat_l, :])])
        s1[d, stat_m, :] = peak
        s1[d, stat_l, :] = total
        cols = [jnp.transpose(f) for f in fac]
        for seq in range(seqs):
            at = pl.ds(seq * q_heads, q_heads)
            s1[d, at, :] = (o_ref[core, piece, at, :] * cols[0][:q_heads, seq:seq + 1]
                            + r1[d, at, :] * cols[1][:q_heads, seq:seq + 1])
        if d:
            in2[d] = send(s1.at[d], r2.at[d], b_s.at[d], b_r.at[d], peer1(d))
    for d in order:
        in2[d].wait_recv()
    peak, total, fac = blend([(s1[0, stat_m, :], s1[0, stat_l, :])] + [(r2[d, stat_m, :], r2[d, stat_l, :]) for d in range(1, side)])
    cols = [jnp.transpose(f) for f in fac]
    for k in range(side):
        for i in range(2):
            seq = 2 * k + i
            at = pl.ds(seq * q_heads, q_heads)
            value = s1[0, at, :] * cols[0][:q_heads, seq:seq + 1]
            for d in range(1, side):
                value += r2[d, at, :] * cols[d][:q_heads, seq:seq + 1]
            s2[k, pl.ds(i * q_heads, q_heads), :] = value
        s2[k, pl.ds(rows, seqs), :] = peak
        s2[k, pl.ds(rows + seqs, seqs), :] = total
    in3 = {}
    for d in order:
        in3[d] = send(s2.at[lax.rem(second + d, side)], r3.at[d], c_s.at[d], c_r.at[d], peer2(d))
    for d in order:
        in3[d].wait_recv()
    low, high = pl.ds(rows, seqs), pl.ds(rows + seqs, seqs)
    peak, total, fac = blend([(s2[0, low, :], s2[0, high, :])] + [(r3[d, low, :], r3[d, high, :]) for d in range(1, side)])
    for n, tile in enumerate(fac + [total]):
        fin[n] = tile
    mine = pl.ds(2 * second, 2)
    cols = [jnp.transpose(jnp.concatenate([fin[n, mine, :]] * (seqs // 2), axis=0)) for n in range(side + 1)]
    for i in range(2):
        at = pl.ds(i * q_heads, q_heads)
        value = s2[second, at, :] * cols[0][:q_heads, i:i + 1]
        for d in range(1, side):
            value += r3[d, at, :] * cols[d][:q_heads, i:i + 1]
        value = value / cols[side][:q_heads, i:i + 1]
        obuf[pl.ds(pl.multiple_of(core * rows, 8) + i * q_heads, q_heads), :] = value.astype(BF16).astype(F32)
    own = obuf.at[pl.ds(pl.multiple_of(core * rows, 8), rows)]
    swap = send(own, own, d_s, d_r, partner)
    lhs[...] = jnp.zeros_like(lhs)
    for copy in w_copies:
        copy.wait()
    swap.wait_recv()
    for h in range(q_heads):
        lhs[0:4, h * head_dim:(h + 1) * head_dim] = obuf[pl.ds(h, 4, stride=q_heads), :]
    left = lhs[...].astype(BF16)
    n_step = 512
    for n in range(0, width, n_step):
        gbuf[core, second, first, :, n:n + n_step] = jnp.dot(left, wbuf[:, n:n + n_step], preferred_element_type=F32)[0:4]

    def block(s, f):
        return gbuf.at[core, s, f]

    g1, g2, g3 = {}, {}, {}
    for d in order:
        g1[d] = send(block(second, first), block(second, first), e_s.at[d], e_r.at[d], peer1(d))
    for e in order:
        g2[e, 0] = send(block(second, first), block(second, first), f_s.at[e, 0], f_r.at[e, 0], peer2(e))
    for d in order[1:] + order[:1]:
        f_from = lax.rem(first - d + side, side)
        g1[d].wait_recv()
        for e in order:
            g2[e, d] = send(block(second, f_from), block(second, f_from), f_s.at[e, d], f_r.at[e, d], peer2(e))
    g3[0] = send(gbuf.at[core, second], gbuf.at[core, second], h_s.at[0], h_r.at[0], partner)
    for e in order[1:] + order[:1]:
        s_from = lax.rem(second - e + side, side)
        for d in range(side):
            g2[e, d].wait_recv()
        g3[e] = send(gbuf.at[core, s_from], gbuf.at[core, s_from], h_s.at[e], h_r.at[e], partner)
    for key in g3:
        g3[key].wait_recv()
    for half in range(2):
        at = slice(half * width, (half + 1) * width)
        for s in range(side):
            for f in range(side):
                px, py = (f, s) if half == 0 else (s, f)
                a = 2 * (px * side + py)
                b = 2 * (side * side + py * side + px)
                out_ref[a:a + 2, at] = gbuf[half, s, f, 0:2]
                out_ref[b:b + 2, at] = gbuf[half, s, f, 2:4]

    for group in (in1, in2, in3, g1, g2, g3):
        for copy in group.values():
            copy.wait_send()
    swap.wait_send()


def combine(part, tokens, w_o, side):
    seq_count, dim = tokens.shape
    steps, part_rows, head_dim = part.shape
    seqs = seq_count // steps
    q_heads = part_rows // seqs - 2
    parts = part.reshape(2, side, part_rows, head_dim)
    width = dim // 2
    depth = w_o.shape[0]
    dma = pltpu.SemaphoreType.DMA
    hbm = pl.BlockSpec(memory_space=pl.ANY)
    piece = (side, part_rows, head_dim)
    small = (side, 2 * q_heads + 2 * seqs, head_dim)
    return pl.pallas_call(
        functools.partial(combine_body, side, q_heads, seqs),
        out_shape=jax.ShapeDtypeStruct(tokens.shape, F32),
        in_specs=[pl.BlockSpec(memory_space=pltpu.VMEM), hbm],
        out_specs=pl.BlockSpec(memory_space=pltpu.VMEM),
        scratch_shapes=[
            pltpu.VMEM(piece, F32), pltpu.VMEM(piece, F32), pltpu.VMEM(piece, F32),
            pltpu.VMEM(small, F32), pltpu.VMEM(small, F32),
            pltpu.VMEM((side + 1, seqs, head_dim), F32),
            pltpu.VMEM((4 * q_heads, head_dim), F32),
            pltpu.VMEM((8, depth), F32),
            pltpu.VMEM((depth, width), BF16),
            pltpu.VMEM((2, side, side, 4, width), F32),
            dma((4,)),
            dma((side,)), dma((side,)),
            dma((side,)), dma((side,)),
            dma((side,)), dma((side,)),
            dma, dma,
            dma((side,)), dma((side,)),
            dma((side, side)), dma((side, side)),
            dma((side,)), dma((side,)),
        ],
        compiler_params=pltpu.CompilerParams(collective_id=1, has_side_effects=True, vmem_limit_bytes=LIMIT_C),
        name="combine",
    )(parts, w_o)


def solution(mesh):
    cache_spec = P('dp', 'sp', None, None)
    side = int(round((mesh.shape['sp'] // 2) ** 0.5))

    def device_step(tokens, positions, k_cache, v_cache, w_q, w_k, w_v, w_o, attn_norm, q_norm, k_norm):
        seq_count, slots, kv_heads, head_dim = k_cache.shape
        shard_start = (lax.axis_index('sp') * slots).astype(jnp.int32).reshape(1)
        seqs = 8
        heads = project(seqs, tokens, positions, w_q, w_k, w_v, attn_norm, q_norm, k_norm)
        k_upd, v_upd, part, new_kv = attention(seqs, heads, positions, shard_start, k_cache, v_cache)
        mixed = combine(part, tokens, w_o, side)
        block_out = (tokens.astype(F32) + mixed).astype(BF16)
        return block_out, k_upd, v_upd, new_kv

    return jax.shard_map(device_step, mesh=mesh, in_specs=(P('dp', None), P('dp'), cache_spec, cache_spec, P(), P(), P(), P(), P(), P(), P()), out_specs=(P('dp', None), cache_spec, cache_spec, P('dp', None, None, None)), check_vma=False)
```

time: 262 us -> 66.1 us (0.25)
  waiting for transfers between devices: 98.7 us -> 0 us
  Pallas kernels: 0 us -> 64.3 us
  matrix products: 61.1 us -> 0 us
  blocking collectives: 51.5 us -> 0 us
  other arithmetic: 24 us -> 0.95 us
  between operations: 14.3 us -> 0.73 us
  local copies, waits for them, and re-layouts: 12.4 us -> 0.02 us
    psum x1 -> x0, waiting for transfers between devices: 98.7 us -> none  [device_step(): summed = lax.psum(packed, 'sp')]
    pallas_call x0 -> x3, Pallas kernels: none -> 64.3 us  [the longest x1 34.2 us: combine(): pl.pallas_call(functools.partial(combine_body, side, q_heads, seqs), out_...]
    dot_general x6 -> x0, matrix products: 61.1 us -> none  [the longest x1 21.5 us: device_step(): jnp.dot(attn_out, w_o, preferred_element_type=jnp.float32)]
    pmax x1 -> x0, blocking collectives: 51.5 us -> none  [device_step(): global_peak = lax.pmax(local_peak, 'sp')]
    select_n x1 -> x0, other arithmetic: 9.47 us -> none  [local_attention(): v_upd = jnp.where(write_mask, v_new[:, None], v_loc)]
    broadcast_in_dim x1 -> x0, local copies, waits for them, and re-layouts: 5.42 us -> none  [device_step(): (local_sum * factor)[..., None]]
    convert_element_type x5 -> x1, other arithmetic: 4.64 us -> 0.95 us  [device_step(): block_out = (tokens.astype(F32) + mixed).astype(BF16)]
    reduce_sum x4 -> x0, other arithmetic: 3.35 us -> none  [the longest x3 2.01 us: rms_scale(): jnp.mean(values * values, axis=-1, keepdims=True) + NORM_EPS]
  transfers between devices with their start and end apart: 1 -> 0, of which waited for: 1 -> 0; matrix products, arithmetic and copies ran while one was open for 0% -> 0% of each run, Pallas kernels for 0% -> 0%
where the time goes in v3:
time: 66.1 us; the launch traced here: 66 us
  Pallas kernels  64.3 us (97%)
  other arithmetic  0.95 us (1%)
  between operations  0.73 us (1%)
    pallas_call x1, Pallas kernels, combine(): pl.pallas_call(functools.partial(combine_body, side, q_heads, seqs), out_...  34.2 us
    pallas_call x1, Pallas kernels, project(): pl.pallas_call(functools.partial(project_body, seq_count, q_heads, kv_hea...  20.4 us
    pallas_call x1, Pallas kernels, attention(): pl.pallas_call(functools.partial(attn_body, steps, seqs, slots, kv_heads,...  9.64 us

profile of v3, /device:TPU:97, one launch (start us, length us, event | category | flops | bytes accessed | tf_op | source)
XLA Modules:
  0.0 66.0 jit_solution(6591086608795458375)
XLA Ops:
  0.6 0.0 copy-start
  0.6 0.0 copy-start.1
  0.7 0.0 copy-start.2
  0.7 20.4 %project.1.heads = f32[8,56,8,128]{3,2,1,0:T(8,128)S(1)} custom-call(bf16[64,5120]{1,0:T(8,128)(2,1)} %tok_ref.1, bf16[40,128]{1,0:T(8,128)(2,1)} %bitcast.15, bf16[1,128]{1,0:T(2,128)(2,1)} %bitcast.16, bf16[1,128]{1,0:T(2,128)(2,1)} %bitcast.17, s32[1,64]{1,0:T(1,128)} %bitcast.14, f32[1,128]{1,0:T(1,128)} %constant.9.freq_ref, bf16[5120,5120]{1,0:T(8,128)(2,1)} %wq_ref.1, ...), custom_call_target="tpu_custom_call" | custom-call | tf_op jit(solution)/shard_map/project/pallas_call | solution.py:123
  21.1 0.0 copy-done
  21.1 0.0 copy-done.1
  21.1 0.0 copy-done.2
  21.1 9.6 %attend.1 = (bf16[64,32,16,128]{3,2,1,0:T(8,128)(2,1)}, bf16[64,32,16,128]{3,2,1,0:T(8,128)(2,1)}, f32[8,336,128]{2,1,0:T(8,128)S(1)}, bf16[64,16,128]{2,1,0:T(8,128)(2,1)}) custom-call(s32[64]{0:T(128)S(1)} %copy-done.2, s32[1]{0:T(128)} %bitcast.start_ref, f32[8,56,8,128]{3,2,1,0:T(8,128)S(1)} %project.1.heads, bf16[64,32,16,128]{3,2,1,0:T(8,128)(2,1)S(1)} %bitcast.11, ...), custom_call_target="tpu_custom_call" | custom-call | tf_op jit(solution)/shard_map/attend/pallas_call | solution.py:245
  30.8 0.0 copy-start.3
  30.8 34.2 %combine.1 = f32[64,5120]{1,0:T(8,128)S(1)} custom-call(f32[2,4,336,128]{3,2,1,0:T(8,128)S(1)} %bitcast.13, bf16[5120,5120]{1,0:T(8,128)(2,1)} %wo_ref.1), custom_call_target="tpu_custom_call" | custom-call | tf_op jit(solution)/shard_map/combine/pallas_call | solution.py:437
  65.0 0.0 copy-done.3
  65.0 0.9 %add_convert_fusion = bf16[64,5120]{1,0:T(8,128)(2,1)} fusion(f32[64,5120]{1,0:T(8,128)S(1)} %combine.1, bf16[64,5120]{1,0:T(8,128)(2,1)S(1)} %copy-done.3), kind=kLoop, calls=%fused_computation | loop fusion | flops 983040 | bytes 2621440 | tf_op jit(solution)/shard_map/convert_element_type | solution.py:475
Async XLA Ops:
  0.6 20.5 %copy-start = (bf16[64,64,8,128]{3,2,1,0:T(8,128)(2,1)S(1)}, bf16[64,64,8,128]{3,2,1,0:T(8,128)(2,1)}, u32[]{:S(2)}) copy-start(bf16[64,64,8,128]{3,2,1,0:T(8,128)(2,1)} %param.14) | copy-start | bytes 25165828
  0.6 20.5 %copy-start.1 = (bf16[64,64,8,128]{3,2,1,0:T(8,128)(2,1)S(1)}, bf16[64,64,8,128]{3,2,1,0:T(8,128)(2,1)}, u32[]{:S(2)}) copy-start(bf16[64,64,8,128]{3,2,1,0:T(8,128)(2,1)} %param.15) | copy-start | bytes 25165828
  0.7 20.5 %copy-start.2 = (s32[64]{0:T(128)S(1)}, s32[64]{0:T(128)}, u32[]{:S(2)}) copy-start(s32[64]{0:T(128)} %pos_ref.1) | copy-start | bytes 772
  30.8 34.3 %copy-start.3 = (bf16[64,5120]{1,0:T(8,128)(2,1)S(1)}, bf16[64,5120]{1,0:T(8,128)(2,1)}, u32[]{:S(2)}) copy-start(bf16[64,5120]{1,0:T(8,128)(2,1)} %tok_ref.1) | copy-start | bytes 1966084

commit v4 on v3

--- a/solution.py
+++ b/solution.py
@@ -51,7 +51,7 @@
     load = pltpu.make_async_copy(tok_ref, tok, t_sem)
     load.start()
     pieces = [(i, j) for i in range(chunks) for j in range(splits)]
-    ahead = 3
+    ahead = 5
     for i, j in pieces[:ahead]:
         fetch(i, j).start()
 
@@ -278,7 +278,7 @@
     return peak, total, factors
 
 
-def combine_body(side, q_heads, seqs, o_ref, wo_ref, out_ref, r1, s1, r2, s2, r3, fin, obuf, lhs, wbuf, gbuf,
+def combine_body(side, q_heads, seqs, o_ref, wo_ref, out_ref, r1, s1, r2, s2, r3, fin, obuf, lhs, wbuf, gbuf0, gbuf1,
                  w_sem, a_s, a_r, b_s, b_r, c_s, c_r, d_s, d_r, e_s, e_r, f_s, f_r, h_s, h_r):
     me = lax.axis_index("sp")
     core = lax.rem(me, 2)
@@ -291,6 +291,7 @@
     stride2 = 2 * side * (1 - core) + 2 * core
     partner = me + 1 - 2 * core
     head_dim = o_ref.shape[-1]
+    gbufs = (gbuf0, gbuf1)
     depth, width = wbuf.shape
     w_parts = w_sem.shape[0]
     w_rows = depth // w_parts
@@ -381,40 +382,47 @@
     for h in range(q_heads):
         lhs[0:4, h * head_dim:(h + 1) * head_dim] = obuf[pl.ds(h, 4, stride=q_heads), :]
     left = lhs[...].astype(BF16)
+    g1, g2, g3 = {}, {}, {}
     n_step = 512
-    for n in range(0, width, n_step):
-        gbuf[core, second, first, :, n:n + n_step] = jnp.dot(left, wbuf[:, n:n + n_step], preferred_element_type=F32)[0:4]
-
-    def block(s, f):
-        return gbuf.at[core, s, f]
-
-    g1, g2, g3 = {}, {}, {}
-    for d in order:
-        g1[d] = send(block(second, first), block(second, first), e_s.at[d], e_r.at[d], peer1(d))
-    for e in order:
-        g2[e, 0] = send(block(second, first), block(second, first), f_s.at[e, 0], f_r.at[e, 0], peer2(e))
-    for d in order[1:] + order[:1]:
-        f_from = lax.rem(first - d + side, side)
-        g1[d].wait_recv()
+    done = 0
+    for q, gbuf in enumerate(gbufs):
+        own = gbuf.at[core, second, first]
+        for n in range(0, gbuf.shape[-1], n_step):
+            gbuf[core, second, first, :, n:n + n_step] = jnp.dot(left, wbuf[:, done + n:done + n + n_step], preferred_element_type=F32)[0:4]
+        done += gbuf.shape[-1]
+        for d in order:
+            g1[q, d] = send(own, own, e_s.at[q, d], e_r.at[q, d], peer1(d))
         for e in order:
-            g2[e, d] = send(block(second, f_from), block(second, f_from), f_s.at[e, d], f_r.at[e, d], peer2(e))
-    g3[0] = send(gbuf.at[core, second], gbuf.at[core, second], h_s.at[0], h_r.at[0], partner)
-    for e in order[1:] + order[:1]:
-        s_from = lax.rem(second - e + side, side)
-        for d in range(side):
-            g2[e, d].wait_recv()
-        g3[e] = send(gbuf.at[core, s_from], gbuf.at[core, s_from], h_s.at[e], h_r.at[e], partner)
-    for key in g3:
-        g3[key].wait_recv()
-    for half in range(2):
-        at = slice(half * width, (half + 1) * width)
-        for s in range(side):
-            for f in range(side):
-                px, py = (f, s) if half == 0 else (s, f)
-                a = 2 * (px * side + py)
-                b = 2 * (side * side + py * side + px)
-                out_ref[a:a + 2, at] = gbuf[half, s, f, 0:2]
-                out_ref[b:b + 2, at] = gbuf[half, s, f, 2:4]
+            g2[q, e, 0] = send(own, own, f_s.at[q, e, 0], f_r.at[q, e, 0], peer2(e))
+    for q, gbuf in enumerate(gbufs):
+        for d in order[1:] + order[:1]:
+            f_from = lax.rem(first - d + side, side)
+            got = gbuf.at[core, second, f_from]
+            g1[q, d].wait_recv()
+            for e in order:
+                g2[q, e, d] = send(got, got, f_s.at[q, e, d], f_r.at[q, e, d], peer2(e))
+        row = gbuf.at[core, second]
+        g3[q, 0] = send(row, row, h_s.at[q, 0], h_r.at[q, 0], partner)
+    for q, gbuf in enumerate(gbufs):
+        for e in order[1:] + order[:1]:
+            row = gbuf.at[core, lax.rem(second - e + side, side)]
+            for d in range(side):
+                g2[q, e, d].wait_recv()
+            g3[q, e] = send(row, row, h_s.at[q, e], h_r.at[q, e], partner)
+    done = 0
+    for q, gbuf in enumerate(gbufs):
+        for e in range(side):
+            g3[q, e].wait_recv()
+        for half in range(2):
+            at = slice(half * width + done, half * width + done + gbuf.shape[-1])
+            for s in range(side):
+                for f in range(side):
+                    px, py = (f, s) if half == 0 else (s, f)
+                    a = 2 * (px * side + py)
+                    b = 2 * (side * side + py * side + px)
+                    out_ref[a:a + 2, at] = gbuf[half, s, f, 0:2]
+                    out_ref[b:b + 2, at] = gbuf[half, s, f, 2:4]
+        done += gbuf.shape[-1]
 
     for group in (in1, in2, in3, g1, g2, g3):
         for copy in group.values():
@@ -429,6 +437,7 @@
     q_heads = part_rows // seqs - 2
     parts = part.reshape(2, side, part_rows, head_dim)
     width = dim // 2
+    near = width * 3 // 5 // 512 * 512
     depth = w_o.shape[0]
     dma = pltpu.SemaphoreType.DMA
     hbm = pl.BlockSpec(memory_space=pl.ANY)
@@ -446,15 +455,16 @@
             pltpu.VMEM((4 * q_heads, head_dim), F32),
             pltpu.VMEM((8, depth), F32),
             pltpu.VMEM((depth, width), BF16),
-            pltpu.VMEM((2, side, side, 4, width), F32),
+            pltpu.VMEM((2, side, side, 4, near), F32),
+            pltpu.VMEM((2, side, side, 4, width - near), F32),
             dma((4,)),
             dma((side,)), dma((side,)),
             dma((side,)), dma((side,)),
             dma((side,)), dma((side,)),
             dma, dma,
-            dma((side,)), dma((side,)),
-            dma((side, side)), dma((side, side)),
-            dma((side,)), dma((side,)),
+            dma((2, side)), dma((2, side)),
+            dma((2, side, side)), dma((2, side, side)),
+            dma((2, side)), dma((2, side)),
         ],
         compiler_params=pltpu.CompilerParams(collective_id=1, has_side_effects=True, vmem_limit_bytes=LIMIT_C),
         name="combine",

time: 66.1 us -> 63 us (0.953)
  Pallas kernels: 64.3 us -> 61.3 us
    pallas_call x1, Pallas kernels: 34.2 us -> 32.5 us  [combine(): pl.pallas_call(functools.partial(combine_body, side, q_heads, seqs), out_...]
    pallas_call x1, Pallas kernels: 20.4 us -> 19.1 us  [project(): pl.pallas_call(functools.partial(project_body, seq_count, q_heads, kv_hea...]
where the time goes in v4:
time: 63 us
  Pallas kernels  61.3 us (97%)
  other arithmetic  0.95 us (2%)
  between operations  0.73 us (1%)
    pallas_call x1, Pallas kernels, combine(): pl.pallas_call(functools.partial(combine_body, side, q_heads, seqs), out_...  32.5 us
    pallas_call x1, Pallas kernels, project(): pl.pallas_call(functools.partial(project_body, seq_count, q_heads, kv_hea...  19.1 us
    pallas_call x1, Pallas kernels, attention(): pl.pallas_call(functools.partial(attn_body, steps, seqs, slots, kv_heads,...  9.65 us

profile of v4, /device:TPU:97, one launch (start us, length us, event | category | flops | bytes accessed | tf_op | source)
XLA Modules:
  0.0 63.0 jit_solution(5634090901265229962)
XLA Ops:
  0.6 0.0 copy-start
  0.6 0.0 copy-start.1
  0.7 0.0 copy-start.2
  0.7 19.1 %project.1.heads = f32[8,56,8,128]{3,2,1,0:T(8,128)S(1)} custom-call(bf16[64,5120]{1,0:T(8,128)(2,1)} %tok_ref.1, bf16[40,128]{1,0:T(8,128)(2,1)} %bitcast.15, bf16[1,128]{1,0:T(2,128)(2,1)} %bitcast.16, bf16[1,128]{1,0:T(2,128)(2,1)} %bitcast.17, s32[1,64]{1,0:T(1,128)} %bitcast.14, f32[1,128]{1,0:T(1,128)} %constant.9.freq_ref, bf16[5120,5120]{1,0:T(8,128)(2,1)} %wq_ref.1, ...), custom_call_target="tpu_custom_call" | custom-call | tf_op jit(solution)/shard_map/project/pallas_call | solution.py:123
  19.8 0.0 copy-done
  19.8 0.0 copy-done.1
  19.8 0.0 copy-done.2
  19.8 9.6 %attend.1 = (bf16[64,32,16,128]{3,2,1,0:T(8,128)(2,1)}, bf16[64,32,16,128]{3,2,1,0:T(8,128)(2,1)}, f32[8,336,128]{2,1,0:T(8,128)S(1)}, bf16[64,16,128]{2,1,0:T(8,128)(2,1)}) custom-call(s32[64]{0:T(128)S(1)} %copy-done.2, s32[1]{0:T(128)} %bitcast.start_ref, f32[8,56,8,128]{3,2,1,0:T(8,128)S(1)} %project.1.heads, bf16[64,32,16,128]{3,2,1,0:T(8,128)(2,1)S(1)} %bitcast.11, ...), custom_call_target="tpu_custom_call" | custom-call | tf_op jit(solution)/shard_map/attend/pallas_call | solution.py:245
  29.4 0.0 copy-start.3
  29.4 32.5 %combine.1 = f32[64,5120]{1,0:T(8,128)S(1)} custom-call(f32[2,4,336,128]{3,2,1,0:T(8,128)S(1)} %bitcast.13, bf16[5120,5120]{1,0:T(8,128)(2,1)} %wo_ref.1), custom_call_target="tpu_custom_call" | custom-call | tf_op jit(solution)/shard_map/combine/pallas_call | solution.py:446
  62.0 0.0 copy-done.3
  62.0 0.9 %add_convert_fusion = bf16[64,5120]{1,0:T(8,128)(2,1)} fusion(f32[64,5120]{1,0:T(8,128)S(1)} %combine.1, bf16[64,5120]{1,0:T(8,128)(2,1)S(1)} %copy-done.3), kind=kLoop, calls=%fused_computation | loop fusion | flops 983040 | bytes 2621440 | tf_op jit(solution)/shard_map/convert_element_type | solution.py:485
Async XLA Ops:
  0.6 19.1 %copy-start = (bf16[64,64,8,128]{3,2,1,0:T(8,128)(2,1)S(1)}, bf16[64,64,8,128]{3,2,1,0:T(8,128)(2,1)}, u32[]{:S(2)}) copy-start(bf16[64,64,8,128]{3,2,1,0:T(8,128)(2,1)} %param.14) | copy-start | bytes 25165828
  0.6 19.1 %copy-start.1 = (bf16[64,64,8,128]{3,2,1,0:T(8,128)(2,1)S(1)}, bf16[64,64,8,128]{3,2,1,0:T(8,128)(2,1)}, u32[]{:S(2)}) copy-start(bf16[64,64,8,128]{3,2,1,0:T(8,128)(2,1)} %param.15) | copy-start | bytes 25165828
  0.7 19.1 %copy-start.2 = (s32[64]{0:T(128)S(1)}, s32[64]{0:T(128)}, u32[]{:S(2)}) copy-start(s32[64]{0:T(128)} %pos_ref.1) | copy-start | bytes 772
  29.4 32.6 %copy-start.3 = (bf16[64,5120]{1,0:T(8,128)(2,1)S(1)}, bf16[64,5120]{1,0:T(8,128)(2,1)}, u32[]{:S(2)}) copy-start(bf16[64,5120]{1,0:T(8,128)(2,1)} %tok_ref.1) | copy-start | bytes 1966084

commit v5 on v4

--- a/solution.py
+++ b/solution.py
@@ -42,11 +42,13 @@
         own = side * (q_heads // 2) + (i - 2 * kv_chunks) * per
         return 2 * kv_heads + own, wq_ref, own
 
-    def fetch(i, j):
-        _, ref, head = first_head(i, core)
+    sequence = list(range(2 * kv_chunks, chunks)) + list(range(2 * kv_chunks))
+
+    def fetch(n, j):
+        _, ref, head = first_head(sequence[n], core)
         return pltpu.make_async_copy(
             ref.at[pl.ds(j * rows, rows), pl.ds(pl.multiple_of(head * head_dim, 128), width)],
-            wbuf.at[i % slots, pl.ds(j * rows, rows), :], w_sem.at[i, j])
+            wbuf.at[n % slots, pl.ds(j * rows, rows), :], w_sem.at[n, j])
 
     load = pltpu.make_async_copy(tok_ref, tok, t_sem)
     load.start()
@@ -77,14 +79,14 @@
 
     swaps = []
     blocks, _, block, _ = heads.shape
-    for i in range(chunks):
+    for turn, i in enumerate(sequence):
         acc = None
         for j in range(splits):
-            at = i * splits + j
-            fetch(i, j).wait()
+            at = turn * splits + j
+            fetch(turn, j).wait()
             if at + ahead < len(pieces):
                 fetch(*pieces[at + ahead]).start()
-            part = jnp.dot(hid[:, j * rows:(j + 1) * rows], wbuf[i % slots, j * rows:(j + 1) * rows, :], preferred_element_type=F32)
+            part = jnp.dot(hid[:, j * rows:(j + 1) * rows], wbuf[turn % slots, j * rows:(j + 1) * rows, :], preferred_element_type=F32)
             acc = part if acc is None else acc + part
         acc = acc.astype(BF16).astype(F32)
         at = first_head(i, core)[0]
@@ -138,21 +140,21 @@
 
 
 def attn_body(steps, seqs, slots, kv_heads, q_heads, pos_ref, start_ref, heads, k_ref, v_ref, ko_ref, vo_ref, obuf, nk_ref,
-              kbuf, vbuf, nkbuf, sc_ref, pw_ref, o_sem):
+              kbuf0, kbuf1, kbuf2, vbuf0, vbuf1, vbuf2, nkbuf, sc_ref, pw_ref, o_sem):
     head_dim = k_ref.shape[-1]
     scale = head_dim ** -0.5
     cols = slots * kv_heads
     group = q_heads // kv_heads
     o_rows = seqs * q_heads
+    kbufs, vbufs = (kbuf0, kbuf1, kbuf2), (vbuf0, vbuf1, vbuf2)
 
     def span(i):
         return pl.ds(i * seqs, seqs)
 
     def caches_out(i):
-        slot = lax.rem(i, 2)
         return [
-            pltpu.make_async_copy(kbuf.at[slot], ko_ref.at[span(i)], o_sem.at[i, 2]),
-            pltpu.make_async_copy(vbuf.at[slot], vo_ref.at[span(i)], o_sem.at[i, 3]),
+            pltpu.make_async_copy(kbufs[i % 3], ko_ref.at[span(i)], o_sem.at[i, 2]),
+            pltpu.make_async_copy(vbufs[i % 3], vo_ref.at[span(i)], o_sem.at[i, 3]),
         ]
 
     def rest_out(i):
@@ -171,43 +173,45 @@
     diag_c = lax.broadcasted_iota(jnp.int32, (q_heads, head_dim), 1)
     diag = diag_r == diag_c
 
-    @pl.loop(0, steps)
-    def _(i):
+    def bring(i, b):
+        kbufs[i % 3][b] = k_ref[i * seqs + b]
+        vbufs[i % 3][b] = v_ref[i * seqs + b]
+
+    for b in range(seqs):
+        bring(0, b)
+    for i in range(steps):
+        kbuf, vbuf = kbufs[i % 3], vbufs[i % 3]
         rows_of = heads.at[i].reshape((2 * kv_heads + q_heads) * seqs, head_dim)
-        slot = lax.rem(i, 2)
-
-        @pl.when(i >= 2)
-        def _():
+        if i >= 2:
             for copy in caches_out(i - 2):
                 copy.wait()
-
         for b in range(seqs):
             rel = pos_ref[i * seqs + b] - start_ref[0]
             at = i * seqs + b
-            kbuf[slot, b] = k_ref[at]
-            vbuf[slot, b] = v_ref[at]
             k_new = rows_of[pl.ds(b, kv_heads, stride=seqs), :]
             v_new = rows_of[pl.ds(b + kv_heads * seqs, kv_heads, stride=seqs), :]
             nkbuf[at] = jnp.concatenate([k_new, v_new], axis=0).astype(BF16)
 
             @pl.when((rel >= 0) & (rel < slots))
-            def _():
+            def _(b=b, rel=rel, k_new=k_new, v_new=v_new, kbuf=kbuf, vbuf=vbuf):
                 tile = lax.div(rel, 2)
                 hit = upper == (lax.rem(rel, 2) == 1)
                 k_two = jnp.concatenate([k_new, k_new], axis=0)
                 v_two = jnp.concatenate([v_new, v_new], axis=0)
-                kbuf[slot, b, tile] = jnp.where(hit, k_two, kbuf[slot, b, tile].astype(F32)).astype(BF16)
-                vbuf[slot, b, tile] = jnp.where(hit, v_two, vbuf[slot, b, tile].astype(F32)).astype(BF16)
+                kbuf[b, tile] = jnp.where(hit, k_two, kbuf[b, tile].astype(F32)).astype(BF16)
+                vbuf[b, tile] = jnp.where(hit, v_two, vbuf[b, tile].astype(F32)).astype(BF16)
         for copy in caches_out(i):
             copy.start()
         peaks = []
         for b in range(seqs):
             rel = pos_ref[i * seqs + b] - start_ref[0]
-            keys = kbuf[slot, b].reshape(cols, head_dim)
+            keys = kbuf[b].reshape(cols, head_dim)
             query = rows_of[pl.ds(b + 2 * kv_heads * seqs, q_heads, stride=seqs), :].astype(BF16)
             scores = lax.dot_general(query, keys, (((1,), (1,)), ((), ())), preferred_element_type=F32) * scale
             scores = jnp.where(slot_of <= rel, scores, -jnp.inf)
             sc_ref[b] = scores
+            if i + 1 < steps:
+                bring(i + 1, b)
             peaks.append(jnp.max(scores, axis=1, keepdims=True))
         totals = []
         for b in range(seqs):
@@ -217,7 +221,7 @@
             totals.append(jnp.sum(weights, axis=1, keepdims=True))
             pw_ref[b] = weights.astype(BF16)
         for b in range(seqs):
-            vals = vbuf[slot, b].reshape(cols, head_dim)
+            vals = vbuf[b].reshape(cols, head_dim)
             obuf[i, pl.ds(b * q_heads, q_heads), :] = jnp.dot(pw_ref[b], vals, preferred_element_type=F32)
             peak = jnp.maximum(peaks[b], NEG_FILL)
             obuf[i, pl.ds(o_rows + b, 1), :] = jnp.sum(jnp.where(diag, peak, 0.0), axis=0, keepdims=True)
@@ -253,8 +257,7 @@
             jax.ShapeDtypeStruct((seq_count, 2 * kv_heads, head_dim), BF16),
         ],
         scratch_shapes=[
-            pltpu.VMEM((2, seqs) + k4.shape[1:], BF16),
-            pltpu.VMEM((2, seqs) + v4.shape[1:], BF16),
+            *[pltpu.VMEM((seqs,) + k4.shape[1:], BF16)] * 6,
             pltpu.VMEM((seq_count, 2 * kv_heads, head_dim), BF16),
             pltpu.VMEM((seqs, q_heads, slots * kv_heads), F32),
             pltpu.VMEM((seqs, q_heads, slots * kv_heads), BF16),

time: 63 us -> 62.5 us (level)
  no operation moved by 1% of the time
where the time goes in v5:
time: 62.5 us; the launch traced here: 62.4 us
  Pallas kernels  60.7 us (97%)
  other arithmetic  0.95 us (2%)
  between operations  0.73 us (1%)
    pallas_call x1, Pallas kernels, combine(): pl.pallas_call(functools.partial(combine_body, side, q_heads, seqs), out_...  32.5 us
    pallas_call x1, Pallas kernels, project(): pl.pallas_call(functools.partial(project_body, seq_count, q_heads, kv_hea...  18.9 us
    pallas_call x1, Pallas kernels, attention(): pl.pallas_call(functools.partial(attn_body, steps, seqs, slots, kv_heads,...  9.23 us

profile of v5, /device:TPU:97, one launch (start us, length us, event | category | flops | bytes accessed | tf_op | source)
XLA Modules:
  0.0 62.4 jit_solution(9727342991871872885)
XLA Ops:
  0.6 0.0 copy-start
  0.6 0.0 copy-start.1
  0.7 0.0 copy-start.2
  0.7 18.9 %project.1.heads = f32[8,56,8,128]{3,2,1,0:T(8,128)S(1)} custom-call(bf16[64,5120]{1,0:T(8,128)(2,1)} %tok_ref.1, bf16[40,128]{1,0:T(8,128)(2,1)} %bitcast.15, bf16[1,128]{1,0:T(2,128)(2,1)} %bitcast.16, bf16[1,128]{1,0:T(2,128)(2,1)} %bitcast.17, s32[1,64]{1,0:T(1,128)} %bitcast.14, f32[1,128]{1,0:T(1,128)} %constant.9.freq_ref, bf16[5120,5120]{1,0:T(8,128)(2,1)} %wq_ref.1, ...), custom_call_target="tpu_custom_call" | custom-call | tf_op jit(solution)/shard_map/project/pallas_call | solution.py:125
  19.6 0.0 copy-done
  19.6 0.0 copy-done.1
  19.6 0.0 copy-done.2
  19.6 9.2 %attend.1 = (bf16[64,32,16,128]{3,2,1,0:T(8,128)(2,1)}, bf16[64,32,16,128]{3,2,1,0:T(8,128)(2,1)}, f32[8,336,128]{2,1,0:T(8,128)S(1)}, bf16[64,16,128]{2,1,0:T(8,128)(2,1)}) custom-call(s32[64]{0:T(128)S(1)} %copy-done.2, s32[1]{0:T(128)} %bitcast.start_ref, f32[8,56,8,128]{3,2,1,0:T(8,128)S(1)} %project.1.heads, bf16[64,32,16,128]{3,2,1,0:T(8,128)(2,1)S(1)} %bitcast.11, ...), custom_call_target="tpu_custom_call" | custom-call | tf_op jit(solution)/shard_map/attend/pallas_call | solution.py:249
  28.9 0.0 copy-start.3
  28.9 32.5 %combine.1 = f32[64,5120]{1,0:T(8,128)S(1)} custom-call(f32[2,4,336,128]{3,2,1,0:T(8,128)S(1)} %bitcast.13, bf16[5120,5120]{1,0:T(8,128)(2,1)} %wo_ref.1), custom_call_target="tpu_custom_call" | custom-call | tf_op jit(solution)/shard_map/combine/pallas_call | solution.py:449
  61.4 0.0 copy-done.3
  61.4 0.9 %add_convert_fusion = bf16[64,5120]{1,0:T(8,128)(2,1)} fusion(f32[64,5120]{1,0:T(8,128)S(1)} %combine.1, bf16[64,5120]{1,0:T(8,128)(2,1)S(1)} %copy-done.3), kind=kLoop, calls=%fused_computation | loop fusion | flops 983040 | bytes 2621440 | tf_op jit(solution)/shard_map/convert_element_type | solution.py:488
Async XLA Ops:
  0.6 19.0 %copy-start = (bf16[64,64,8,128]{3,2,1,0:T(8,128)(2,1)S(1)}, bf16[64,64,8,128]{3,2,1,0:T(8,128)(2,1)}, u32[]{:S(2)}) copy-start(bf16[64,64,8,128]{3,2,1,0:T(8,128)(2,1)} %param.14) | copy-start | bytes 25165828
  0.6 19.0 %copy-start.1 = (bf16[64,64,8,128]{3,2,1,0:T(8,128)(2,1)S(1)}, bf16[64,64,8,128]{3,2,1,0:T(8,128)(2,1)}, u32[]{:S(2)}) copy-start(bf16[64,64,8,128]{3,2,1,0:T(8,128)(2,1)} %param.15) | copy-start | bytes 25165828
  0.7 19.0 %copy-start.2 = (s32[64]{0:T(128)S(1)}, s32[64]{0:T(128)}, u32[]{:S(2)}) copy-start(s32[64]{0:T(128)} %pos_ref.1) | copy-start | bytes 772
  28.9 32.6 %copy-start.3 = (bf16[64,5120]{1,0:T(8,128)(2,1)S(1)}, bf16[64,5120]{1,0:T(8,128)(2,1)}, u32[]{:S(2)}) copy-start(bf16[64,5120]{1,0:T(8,128)(2,1)} %tok_ref.1) | copy-start | bytes 1966084
